TPU v7x, 32 devices: a whole 2x2x4 slice. The times are simulated.
32 devices in a mesh: fsdp: 4 (over x, core), ctx: 8 (over z, y).
Axes of the slice: x: 2, y: 2, z: 4, core: 2. Of those that a mesh axis runs over, the one named last changes fastest.
Arguments:
- tokens: bfloat16 [4, 1024, 2048], P('fsdp', 'ctx'), may hold values from -6 to 6
- norm_gain: bfloat16 [2048], P(('fsdp', 'ctx')), may hold values from 0.25 to 1.75
- norm_bias: bfloat16 [2048], P(('fsdp', 'ctx')), may hold values from -3 to 3
- qkv_weight: bfloat16 [2048, 3, 2048], P('ctx', None, 'fsdp'), may hold values from -0.125 to 0.125
- qkv_bias: bfloat16 [3, 2048], P(None, ('fsdp', 'ctx')), may hold values from -7.75 to 7.75
- out_weight: bfloat16 [2048, 2048], P('fsdp', 'ctx'), may hold values from -0.75 to 0.75
- out_bias: bfloat16 [2048], P(('fsdp', 'ctx')), may hold values from -3 to 3
- fc1_weight: bfloat16 [2048, 8192], P('ctx', 'fsdp'), may hold values from -0.125 to 0.125
- fc1_bias: bfloat16 [8192], P(('fsdp', 'ctx')), may hold values from -3 to 3
- fc2_weight: bfloat16 [8192, 2048], P('fsdp', 'ctx'), may hold values from -0.0625 to 0.0625
- fc2_bias: bfloat16 [2048], P(('fsdp', 'ctx')), may hold values from -3 to 3
- cotangent: bfloat16 [4, 1024, 2048], P('fsdp', 'ctx'), may hold values from -6 to 6
Outputs:
- output: bfloat16 [4, 1024, 2048], P('fsdp', 'ctx')
- input_grad: bfloat16 [4, 1024, 2048], P('fsdp', 'ctx')
- grad_norm_gain: float32 [2048], P(('fsdp', 'ctx'))
- grad_norm_bias: float32 [2048], P(('fsdp', 'ctx'))
- grad_qkv_weight: float32 [2048, 3, 2048], P('ctx', None, 'fsdp')
- grad_qkv_bias: float32 [3, 2048], P(None, ('fsdp', 'ctx'))
- grad_out_weight: float32 [2048, 2048], P('fsdp', 'ctx')
- grad_out_bias: float32 [2048], P(('fsdp', 'ctx'))
- grad_fc1_weight: float32 [2048, 8192], P('ctx', 'fsdp')
- grad_fc1_bias: float32 [8192], P(('fsdp', 'ctx'))
- grad_fc2_weight: float32 [8192, 2048], P('fsdp', 'ctx')
- grad_fc2_bias: float32 [2048], P(('fsdp', 'ctx'))
All inputs are finite; a program needn't handle non-finite values.
Results may differ from a plain program's by a relative error of at most 0.03.
The roundings to bfloat16 on the way count: a program that leaves them out, or rounds other values in their place, can miss the bound.
Values may be sent and summed in bfloat16 or wider, within the bound.
A program may use at most 192 MiB of HBM per device.

v0:
```python
import math

import jax
import jax.numpy as jnp
from jax import lax
from jax.sharding import PartitionSpec as P

HEAD_DIM = 64
ROT_DIM = 32


NORM_EPS = 1e-05
GELU_COEF = math.sqrt(2.0 / math.pi)
MASKED = -1e30


def passed_along(value, axis, steps):
    count = lax.axis_size(axis)
    first, last = (max(0, -steps), min(count, count - steps))
    return lax.ppermute(value, axis, [(source, source + steps) for source in range(first, last)])


def passed_along_2(value, axis, steps):
    count = lax.axis_size(axis)
    pairs = [(source, (source + steps) % count) for source in range(count)]
    return lax.ppermute(value, axis, pairs)


def normalize(rows, gain_vec, bias_vec):
    centred = rows - jnp.mean(rows, axis=-1, keepdims=True)
    inv_std = lax.rsqrt(jnp.mean(centred * centred, axis=-1, keepdims=True) + NORM_EPS)
    normed = centred * inv_std
    return (normed * gain_vec.astype(jnp.float32) + bias_vec.astype(jnp.float32), normed, inv_std)


def gelu_tanh(values):
    return (
        0.5 * values * (1.0 + jnp.tanh(GELU_COEF * (values + 0.044715 * values * values * values)))
    )


def gelu_slope(values):
    tangent = jnp.tanh(GELU_COEF * (values + 0.044715 * values * values * values))
    return 0.5 * (1.0 + tangent) + 0.5 * values * (1.0 - tangent * tangent) * GELU_COEF * (
        1.0 + 3.0 * 0.044715 * values * values
    )


def rope_tables(positions, rot_dim):
    half_dim = rot_dim // 2
    inverse = 10000.0 ** (-(jnp.arange(half_dim, dtype=jnp.float32) * 2.0) / rot_dim)
    angles = positions[:, None] * inverse[None, :]
    return (jnp.cos(angles)[:, None, :], jnp.sin(angles)[:, None, :])


def rotate_pairs(values, cosine, sine, rot_dim, sign):
    half_dim = rot_dim // 2
    first_half = values[..., :half_dim]
    second_half = values[..., half_dim:rot_dim]
    return jnp.concatenate(
        [
            first_half * cosine - sign * second_half * sine,
            second_half * cosine + sign * first_half * sine,
            values[..., rot_dim:],
        ],
        axis=-1,
    )


def body(
    tokens,
    norm_gain,
    norm_bias,
    qkv_weight,
    qkv_bias,
    out_weight,
    out_bias,
    fc1_weight,
    fc1_bias,
    fc2_weight,
    fc2_bias,
    cotangent,
):
    f32 = jnp.float32
    bf16 = jnp.bfloat16
    own_seqs, tok_count, width = tokens.shape
    head_dim = HEAD_DIM
    scale = head_dim ** (-0.5)
    local_width = qkv_weight.shape[2]
    local_heads = local_width // head_dim
    own_rows = own_seqs * tok_count
    cycle_size = lax.axis_size("ctx")
    cycle_pos = lax.axis_index("ctx")
    group_pos = lax.axis_index("fsdp")
    gain_full, shift_full, out_bias_full, fc2_bias_full = (
        lax.all_gather(norm_gain, ("fsdp", "ctx"), axis=0, tiled=True),
        lax.all_gather(norm_bias, ("fsdp", "ctx"), axis=0, tiled=True),
        lax.all_gather(out_bias, ("fsdp", "ctx"), axis=0, tiled=True),
        lax.all_gather(fc2_bias, ("fsdp", "ctx"), axis=0, tiled=True),
    )
    tok_all, cot_all = (
        lax.all_gather(tokens, "fsdp", axis=0, tiled=True),
        lax.all_gather(cotangent, "fsdp", axis=0, tiled=True),
    )
    qkv_full, out_full, fc1_full, fc2_full, qkv_bias_full, fc1_bias_full = (
        lax.all_gather(qkv_weight, "ctx", axis=0, tiled=True),
        lax.all_gather(out_weight, "ctx", axis=1, tiled=True),
        lax.all_gather(fc1_weight, "ctx", axis=0, tiled=True),
        lax.all_gather(fc2_weight, "ctx", axis=1, tiled=True),
        lax.all_gather(qkv_bias, "ctx", axis=1, tiled=True),
        lax.all_gather(fc1_bias, "ctx", axis=0, tiled=True),
    )
    seqs = tok_all.shape[0]
    row_count = seqs * tok_count
    query_pos = cycle_pos * tok_count + jnp.arange(tok_count, dtype=jnp.int32)
    query_last = cycle_pos * tok_count + tok_count - 1
    cosine, sine = rope_tables(query_pos.astype(f32), ROT_DIM)
    x_wide = tok_all.reshape(row_count, width).astype(f32)
    normed_out, normed, inv_std = normalize(x_wide, gain_full, shift_full)
    hidden_in = normed_out.astype(bf16)
    mixed = jnp.dot(
        hidden_in, qkv_full.reshape(width, 3 * local_width), preferred_element_type=f32
    ) + qkv_bias_full.reshape(3 * local_width).astype(f32)
    query = rotate_pairs(
        mixed[:, :local_width].reshape(seqs, tok_count, local_heads, head_dim),
        cosine,
        sine,
        ROT_DIM,
        1.0,
    ).astype(bf16)
    key_flat = (
        rotate_pairs(
            mixed[:, local_width : 2 * local_width].reshape(seqs, tok_count, local_heads, head_dim),
            cosine,
            sine,
            ROT_DIM,
            1.0,
        )
        .astype(bf16)
        .reshape(seqs, tok_count, local_width)
    )
    value_flat = mixed[:, 2 * local_width :].astype(bf16).reshape(seqs, tok_count, local_width)
    start_state = (
        jnp.full((seqs, local_heads, tok_count), MASKED, f32),
        jnp.zeros((seqs, local_heads, tok_count), f32),
        jnp.zeros((seqs, tok_count, local_heads, head_dim), f32),
    )
    key_piece = lax.all_gather(key_flat, "ctx", axis=1, tiled=True)
    value_piece = lax.all_gather(value_flat, "ctx", axis=1, tiled=True)
    count = key_piece.shape[1]
    block = math.gcd(count, 512)
    nblocks = count // block
    key_blocks = jnp.moveaxis(key_piece.reshape(seqs, nblocks, block, local_heads, head_dim), 1, 0)
    value_blocks = jnp.moveaxis(
        value_piece.reshape(seqs, nblocks, block, local_heads, head_dim), 1, 0
    )

    def visit(state, item):
        key_blk, value_blk, block_num = item
        first_key = block_num * block

        def update(inner):
            run_max, run_sum, accum = inner
            key_pos = first_key + jnp.arange(block, dtype=jnp.int32)
            allowed = key_pos[None, :] <= query_pos[:, None]
            scores = (
                jnp.einsum("sqhd,skhd->shqk", query, key_blk, preferred_element_type=f32) * scale
            )
            scores = jnp.where(allowed, scores, MASKED)
            new_max = jnp.maximum(run_max, jnp.max(scores, axis=-1))
            factor = jnp.exp(run_max - new_max)
            weights = jnp.where(allowed, jnp.exp(scores - new_max[..., None]), 0.0)
            run_sum = run_sum * factor + jnp.sum(weights, axis=-1)
            accum = accum * jnp.transpose(factor, (0, 2, 1))[..., None]
            accum = accum + jnp.einsum(
                "shqk,skhd->sqhd", weights.astype(bf16), value_blk, preferred_element_type=f32
            )
            return (new_max, run_sum, accum)

        return (lax.cond(first_key <= query_last, update, lambda inner: inner, state), None)

    run_max, run_sum, accum = lax.scan(
        visit, start_state, (key_blocks, value_blocks, jnp.arange(nblocks, dtype=jnp.int32))
    )[0]
    context = accum / jnp.transpose(run_sum, (0, 2, 1))[..., None]
    lse = run_max + jnp.log(run_sum)
    context_b = context.astype(bf16).reshape(row_count, local_width)
    pre = jnp.dot(hidden_in, fc1_full, preferred_element_type=f32) + fc1_bias_full.astype(f32)
    act_b = gelu_tanh(pre).astype(bf16)
    partial_out = jnp.dot(context_b, out_full, preferred_element_type=f32) + jnp.dot(
        act_b, fc2_full, preferred_element_type=f32
    )
    branch_rows = lax.psum_scatter(
        partial_out.astype(jnp.bfloat16), "fsdp", scatter_dimension=0, tiled=True
    ).astype(jnp.float32)
    x_own = tokens.reshape(own_rows, width).astype(f32)
    output = (
        (x_own + branch_rows + out_bias_full.astype(f32) + fc2_bias_full.astype(f32))
        .astype(bf16)
        .reshape(own_seqs, tok_count, width)
    )
    qkv_back, out_back, fc1_back, fc2_back = (
        lax.all_gather(qkv_weight, "ctx", axis=0, tiled=True),
        lax.all_gather(out_weight, "ctx", axis=1, tiled=True),
        lax.all_gather(fc1_weight, "ctx", axis=0, tiled=True),
        lax.all_gather(fc2_weight, "ctx", axis=1, tiled=True),
    )
    grad_rows = cot_all.reshape(row_count, width)
    grad_fc2_w = jnp.dot(act_b.T, grad_rows, preferred_element_type=f32)
    pre_grad = jnp.dot(grad_rows, fc2_back.T, preferred_element_type=f32) * gelu_slope(pre)
    pre_grad_b = pre_grad.astype(bf16)
    grad_fc1_w = jnp.dot(hidden_in.T, pre_grad_b, preferred_element_type=f32)
    grad_fc1_b = jnp.sum(pre_grad, axis=0)
    mlp_back = jnp.dot(pre_grad_b, fc1_back.T, preferred_element_type=f32)
    grad_out_w = jnp.dot(context_b.T, grad_rows, preferred_element_type=f32)
    context_grad = (
        jnp.dot(grad_rows, out_back.T, preferred_element_type=f32)
        .astype(bf16)
        .reshape(seqs, tok_count, local_heads, head_dim)
    )
    delta_rows = jnp.transpose(
        jnp.sum(
            context_grad.astype(f32)
            * context_b.reshape(seqs, tok_count, local_heads, head_dim).astype(f32),
            axis=-1,
        ),
        (0, 2, 1),
    )

    def cycle_step(step_num, state):
        pair, pair_grad, query_grad = state
        source = (cycle_pos - step_num) % cycle_size

        def contribute(inner):
            held_grad, held_query = inner
            key_blk = pair[0].reshape(seqs, tok_count, local_heads, head_dim)
            value_blk = pair[1].reshape(seqs, tok_count, local_heads, head_dim)
            key_pos = source * tok_count + jnp.arange(tok_count, dtype=jnp.int32)
            allowed = key_pos[None, :] <= query_pos[:, None]
            scores = (
                jnp.einsum("sqhd,skhd->shqk", query, key_blk, preferred_element_type=f32) * scale
            )
            probs = jnp.where(allowed, jnp.exp(scores - lse[..., None]), 0.0)
            value_grad = jnp.einsum(
                "shqk,sqhd->skhd", probs.astype(bf16), context_grad, preferred_element_type=f32
            )
            prob_grad = jnp.einsum(
                "sqhd,skhd->shqk", context_grad, value_blk, preferred_element_type=f32
            )
            score_grad = (probs * (prob_grad - delta_rows[..., None])).astype(bf16)
            held_query = (
                held_query
                + jnp.einsum("shqk,skhd->sqhd", score_grad, key_blk, preferred_element_type=f32)
                * scale
            )
            key_grad = (
                jnp.einsum("shqk,sqhd->skhd", score_grad, query, preferred_element_type=f32) * scale
            )
            both = jnp.stack(
                [
                    key_grad.reshape(seqs, tok_count, local_width),
                    value_grad.reshape(seqs, tok_count, local_width),
                ]
            )
            return (held_grad + both, held_query)

        pair_grad, query_grad = lax.cond(
            source <= cycle_pos, contribute, lambda inner: inner, (pair_grad, query_grad)
        )
        pair = passed_along(pair, "ctx", 1)
        pair_grad = passed_along_2(pair_grad.astype(jnp.bfloat16), "ctx", 1).astype(pair_grad.dtype)
        return (pair, pair_grad, query_grad)

    cycle_start = (
        jnp.stack([key_flat, value_flat]),
        jnp.zeros((2, seqs, tok_count, local_width), f32),
        jnp.zeros((seqs, tok_count, local_heads, head_dim), f32),
    )
    final_pair, pair_grad, query_grad = lax.fori_loop(0, cycle_size, cycle_step, cycle_start)
    key_grad = pair_grad[0].reshape(seqs, tok_count, local_heads, head_dim)
    mixed_grad = jnp.concatenate(
        [
            rotate_pairs(query_grad, cosine, sine, ROT_DIM, -1.0).reshape(row_count, local_width),
            rotate_pairs(key_grad, cosine, sine, ROT_DIM, -1.0).reshape(row_count, local_width),
            pair_grad[1].reshape(row_count, local_width),
        ],
        axis=1,
    )
    mixed_grad_b = mixed_grad.astype(bf16)
    grad_qkv_w = jnp.dot(hidden_in.T, mixed_grad_b, preferred_element_type=f32).reshape(
        width, 3, local_width
    )
    grad_qkv_b = jnp.sum(mixed_grad, axis=0).reshape(3, local_width)
    normed_part = (
        jnp.dot(
            mixed_grad_b, qkv_back.reshape(width, 3 * local_width).T, preferred_element_type=f32
        )
        + mlp_back
    )
    normed_grad = lax.psum_scatter(
        normed_part.astype(jnp.bfloat16), "fsdp", scatter_dimension=0, tiled=True
    ).astype(jnp.float32)
    own_start = group_pos * own_rows
    normed_own = lax.dynamic_slice_in_dim(normed, own_start, own_rows, 0)
    inv_std_own = lax.dynamic_slice_in_dim(inv_std, own_start, own_rows, 0)
    cot_own = cotangent.reshape(own_rows, width).astype(f32)
    grad_gain = jnp.sum(normed_grad * normed_own, axis=0)
    grad_shift = jnp.sum(normed_grad, axis=0)
    grad_cot_sum = jnp.sum(cot_own, axis=0)
    hat_grad = normed_grad * gain_full.astype(f32)
    back_rows = inv_std_own * (
        hat_grad
        - jnp.mean(hat_grad, axis=-1, keepdims=True)
        - normed_own * jnp.mean(hat_grad * normed_own, axis=-1, keepdims=True)
    )
    input_grad = (back_rows + cot_own).astype(bf16).reshape(own_seqs, tok_count, width)
    small_shards = (
        lax.psum_scatter(grad_gain, ("fsdp", "ctx"), scatter_dimension=0, tiled=True),
        lax.psum_scatter(grad_shift, ("fsdp", "ctx"), scatter_dimension=0, tiled=True),
        lax.psum_scatter(grad_cot_sum, ("fsdp", "ctx"), scatter_dimension=0, tiled=True),
    )
    all_shards = (
        lax.psum_scatter(
            grad_qkv_w.astype(jnp.bfloat16), "ctx", scatter_dimension=0, tiled=True
        ).astype(jnp.float32),
        lax.psum_scatter(
            grad_qkv_b.astype(jnp.bfloat16), "ctx", scatter_dimension=1, tiled=True
        ).astype(jnp.float32),
        lax.psum_scatter(
            grad_out_w.astype(jnp.bfloat16), "ctx", scatter_dimension=1, tiled=True
        ).astype(jnp.float32),
        lax.psum_scatter(
            grad_fc1_w.astype(jnp.bfloat16), "ctx", scatter_dimension=0, tiled=True
        ).astype(jnp.float32),
        lax.psum_scatter(
            grad_fc1_b.astype(jnp.bfloat16), "ctx", scatter_dimension=0, tiled=True
        ).astype(jnp.float32),
        lax.psum_scatter(
            grad_fc2_w.astype(jnp.bfloat16), "ctx", scatter_dimension=1, tiled=True
        ).astype(jnp.float32),
    )
    shard_qkv_w, shard_qkv_b, shard_out_w, shard_fc1_w, shard_fc1_b, shard_fc2_w = all_shards
    return (
        output,
        input_grad,
        small_shards[0],
        small_shards[1],
        shard_qkv_w,
        shard_qkv_b,
        shard_out_w,
        small_shards[2],
        shard_fc1_w,
        shard_fc1_b,
        shard_fc2_w,
        small_shards[2],
    )


def solution(mesh):
    return jax.shard_map(
        body,
        mesh=mesh,
        in_specs=(
            P("fsdp", "ctx", None),
            P(("fsdp", "ctx")),
            P(("fsdp", "ctx")),
            P("ctx", None, "fsdp"),
            P(None, ("fsdp", "ctx")),
            P("fsdp", "ctx"),
            P(("fsdp", "ctx")),
            P("ctx", "fsdp"),
            P(("fsdp", "ctx")),
            P("fsdp", "ctx"),
            P(("fsdp", "ctx")),
            P("fsdp", "ctx", None),
        ),
        out_specs=(
            P("fsdp", "ctx", None),
            P("fsdp", "ctx", None),
            P(("fsdp", "ctx")),
            P(("fsdp", "ctx")),
            P("ctx", None, "fsdp"),
            P(None, ("fsdp", "ctx")),
            P("fsdp", "ctx"),
            P(("fsdp", "ctx")),
            P("ctx", "fsdp"),
            P(("fsdp", "ctx")),
            P("fsdp", "ctx"),
            P(("fsdp", "ctx")),
        ),
        check_vma=False,
    )
```

profile of v0, /device:TPU:0, one launch (start us, length us, event | category | flops | bytes accessed | tf_op | source)
XLA Modules:
  0.0 1763.8 jit_solution(13420186848989208845)
XLA Ops:
  13.9 43.3 %all-reduce.9 = (bf16[2048]{0:T(1024)(128)(2,1)S(1)}, bf16[2048]{0:T(1024)(128)(2,1)S(1)}, bf16[2048]{0:T(1024)(128)(2,1)}, bf16[2048]{0:T(1024)(128)(2,1)}) all-reduce(bf16[2048]{0:T(1024)(128)(2,1)S(1)} %dynamic-update-slice.1, bf16[2048]{0:T(1024)(128)(2,1)S(1)} %dynamic-update-slice, ...), channel_id=1, replica_groups=mesh['fsdp'=4,'ctx'=8] {'fsdp','ctx'}, use_global_device_ids=true, to_apply=%add.1 | all-reduce | flops 8192 | bytes 32768
  57.2 21.4 %all-gather = bf16[8,64,3]{1,2,0:T(4,128)(2,1)S(1)} all-gather(bf16[1,64,3]{1,2,0:T(4,128)(2,1)S(1)} %bitcast.191), channel_id=1, replica_groups=mesh['fsdp'=4,'ctx'=8] {'ctx'}, dimensions={0}, use_global_device_ids=true | all-gather | bytes 3456 | tf_op jit(solution)/shard_map/all_gather | solution.py:110
  86.1 52.0 %all-gather.13.cloned.1.call-done = bf16[2048,3,512]{0,2,1:T(8,128)(2,1)} async-done(((bf16[256,3,512]{0,2,1:T(8,128)(2,1)}), bf16[2048,3,512]{0,2,1:T(8,128)(2,1)}) %all-gather.13.cloned.1.call-update) | async-done | bytes 6291472 | tf_op jit(solution)/shard_map/all_gather | solution.py:106
  155.7 18.0 %all-gather.1 = bf16[8,1,256]{2,1,0:T(2,128)(2,1)S(1)} all-gather(bf16[1,1,256]{2,1,0:T(2,128)(2,1)S(1)} %reshape.312), channel_id=1, replica_groups=mesh['fsdp'=4,'ctx'=8] {'ctx'}, dimensions={0}, use_global_device_ids=true | all-gather | bytes 4608 | tf_op jit(solution)/shard_map/all_gather | solution.py:111
  176.3 36.4 %all-gather.19.cloned.1.call-done = bf16[512,2048]{1,0:T(8,128)(2,1)} async-done(((bf16[512,256]{1,0:T(8,128)(2,1)}), bf16[512,2048]{1,0:T(8,128)(2,1)}) %all-gather.19.cloned.1.call-update) | async-done | bytes 2097168 | tf_op jit(solution)/shard_map/all_gather | solution.py:107
  224.6 112.8 %all-gather.21.cloned.1.call-done = bf16[2048,2048]{1,0:T(8,128)(2,1)} async-done(((bf16[256,2048]{1,0:T(8,128)(2,1)}), bf16[2048,2048]{1,0:T(8,128)(2,1)}) %all-gather.21.cloned.1.call-update) | async-done | bytes 8388624 | tf_op jit(solution)/shard_map/all_gather | solution.py:108
  348.6 113.8 %all-gather.23.cloned.1.call-done = bf16[2048,2048]{1,0:T(8,128)(2,1)} async-done(((bf16[2048,256]{1,0:T(8,128)(2,1)}), bf16[2048,2048]{1,0:T(8,128)(2,1)}) %all-gather.23.cloned.1.call-update) | async-done | bytes 8388624 | tf_op jit(solution)/shard_map/all_gather | solution.py:109
  462.4 14.2 fusion.72
  476.7 61.2 %all-gather.15.cloned.1.call-done = bf16[4,1024,512]{1,2,0:T(8,128)(2,1)} async-done(((bf16[4,128,512]{1,2,0:T(8,128)(2,1)}), bf16[4,1024,512]{1,2,0:T(8,128)(2,1)}) %all-gather.15.cloned.1.call-update) | async-done | bytes 4194320 | tf_op jit(solution)/shard_map/all_gather | solution.py:148
  551.1 62.3 %all-gather.17.cloned.1.call-done = bf16[4,1024,512]{1,2,0:T(8,128)(2,1)} async-done(((bf16[4,128,512]{1,2,0:T(8,128)(2,1)}), bf16[4,1024,512]{1,2,0:T(8,128)(2,1)}) %all-gather.17.cloned.1.call-update) | async-done | bytes 4194320 | tf_op jit(solution)/shard_map/all_gather | solution.py:149
  640.6 453.7 %while.36 = (s32[]{:T(128)}, bf16[2,4,128,512]{2,3,1,0:T(8,128)(2,1)S(1)}, f32[2,4,128,512]{2,3,1,0:T(8,128)}, f32[4,128,8,64]{1,3,2,0:T(8,128)}, s32[]{:T(128)}...) while((s32[]{:T(128)}, ...), condition=%wide.region_13.14_spmd.clone, body=%wide.region_10.13_spmd.clone.sunk | while | flops 342638848 | bytes 59313760 | solution.py:279
  655.7 30.2 %collective-permute-done.1 = bf16[2,4,128,512]{2,3,1,0:T(8,128)(2,1)S(1)} collective-permute-done((bf16[2,4,128,512]{2,3,1,0:T(8,128)(2,1)}, bf16[2,4,128,512]{2,3,1,0:T(8,128)(2,1)S(1)}, u32[]{:S(2)}, u32[]{:S(2)}) %collective-permute-start.1) | collective-permute-done | bytes 1048608 | tf_op jit(solution)/shard_map/while/body/eval_jaxpr/ppermute | solution.py:26
  702.0 12.6 collective-permute-start.1
  717.7 28.1 %collective-permute-done.1 = bf16[2,4,128,512]{2,3,1,0:T(8,128)(2,1)S(1)} collective-permute-done((bf16[2,4,128,512]{2,3,1,0:T(8,128)(2,1)}, bf16[2,4,128,512]{2,3,1,0:T(8,128)(2,1)S(1)}, u32[]{:S(2)}, u32[]{:S(2)}) %collective-permute-start.1) | collective-permute-done | bytes 1048608 | tf_op jit(solution)/shard_map/while/body/eval_jaxpr/ppermute | solution.py:26
  747.2 11.7 collective-permute-done
  764.4 17.8 %collective-permute-start = (bf16[2,4,128,512]{2,3,1,0:T(8,128)(2,1)S(1)}, bf16[2,4,128,512]{2,3,1,0:T(8,128)(2,1)S(1)}, u32[]{:S(2)}, u32[]{:S(2)}) collective-permute-start(bf16[2,4,128,512]{2,3,1,0:T(8,128)(2,1)S(1)} %copy.171), channel_id=1, source_target_pairs={{0,1},{1,2},{2,3},{3,4},{4,5},{5,6},{6,7},{8,9},{9,10},{10,11},{11... | collective-permute-start | bytes 3145736 | tf_op jit(solution)/shard_map/while/body/eval_jaxpr/ppermute | solution.py:20
  782.2 23.6 %collective-permute-done.1 = bf16[2,4,128,512]{2,3,1,0:T(8,128)(2,1)S(1)} collective-permute-done((bf16[2,4,128,512]{2,3,1,0:T(8,128)(2,1)}, bf16[2,4,128,512]{2,3,1,0:T(8,128)(2,1)S(1)}, u32[]{:S(2)}, u32[]{:S(2)}) %collective-permute-start.1) | collective-permute-done | bytes 1048608 | tf_op jit(solution)/shard_map/while/body/eval_jaxpr/ppermute | solution.py:26
  810.9 15.0 collective-permute-start.1
  831.2 33.7 %collective-permute-done.1 = bf16[2,4,128,512]{2,3,1,0:T(8,128)(2,1)S(1)} collective-permute-done((bf16[2,4,128,512]{2,3,1,0:T(8,128)(2,1)}, bf16[2,4,128,512]{2,3,1,0:T(8,128)(2,1)S(1)}, u32[]{:S(2)}, u32[]{:S(2)}) %collective-permute-start.1) | collective-permute-done | bytes 1048608 | tf_op jit(solution)/shard_map/while/body/eval_jaxpr/ppermute | solution.py:26
  874.1 15.5 collective-permute-start
  889.6 33.6 %collective-permute-done.1 = bf16[2,4,128,512]{2,3,1,0:T(8,128)(2,1)S(1)} collective-permute-done((bf16[2,4,128,512]{2,3,1,0:T(8,128)(2,1)}, bf16[2,4,128,512]{2,3,1,0:T(8,128)(2,1)S(1)}, u32[]{:S(2)}, u32[]{:S(2)}) %collective-permute-start.1) | collective-permute-done | bytes 1048608 | tf_op jit(solution)/shard_map/while/body/eval_jaxpr/ppermute | solution.py:26
  936.9 43.7 %collective-permute-done.1 = bf16[2,4,128,512]{2,3,1,0:T(8,128)(2,1)S(1)} collective-permute-done((bf16[2,4,128,512]{2,3,1,0:T(8,128)(2,1)}, bf16[2,4,128,512]{2,3,1,0:T(8,128)(2,1)S(1)}, u32[]{:S(2)}, u32[]{:S(2)}) %collective-permute-start.1) | collective-permute-done | bytes 1048608 | tf_op jit(solution)/shard_map/while/body/eval_jaxpr/ppermute | solution.py:26
  993.5 43.6 %collective-permute-done.1 = bf16[2,4,128,512]{2,3,1,0:T(8,128)(2,1)S(1)} collective-permute-done((bf16[2,4,128,512]{2,3,1,0:T(8,128)(2,1)}, bf16[2,4,128,512]{2,3,1,0:T(8,128)(2,1)S(1)}, u32[]{:S(2)}, u32[]{:S(2)}) %collective-permute-start.1) | collective-permute-done | bytes 1048608 | tf_op jit(solution)/shard_map/while/body/eval_jaxpr/ppermute | solution.py:26
  1042.9 49.8 %collective-permute-done.1 = bf16[2,4,128,512]{2,3,1,0:T(8,128)(2,1)S(1)} collective-permute-done((bf16[2,4,128,512]{2,3,1,0:T(8,128)(2,1)}, bf16[2,4,128,512]{2,3,1,0:T(8,128)(2,1)S(1)}, u32[]{:S(2)}, u32[]{:S(2)}) %collective-permute-start.1) | collective-permute-done | bytes 1048608 | tf_op jit(solution)/shard_map/while/body/eval_jaxpr/ppermute | solution.py:26
  1159.2 11.6 convolution_convert_fusion
  1173.6 39.9 %all-reduce.7 = bf16[2048]{0:T(1024)(128)(2,1)S(1)} all-reduce(bf16[2048]{0:T(1024)(128)(2,1)S(1)} %copy-done.27), channel_id=11, replica_groups=mesh['fsdp'=4,'ctx'=8] {'ctx'}, use_global_device_ids=true, to_apply=%region_29.30.clone | all-reduce | flops 2048 | bytes 8192
  1226.4 40.6 %all-reduce.8 = (f32[2048]{0:T(1024)S(1)}, f32[2048]{0:T(1024)S(1)}, f32[2048]{0:T(1024)S(1)}) all-reduce(f32[2048]{0:T(1024)S(1)} %get-tuple-element.576, f32[2048]{0:T(1024)S(1)} %get-tuple-element.579, f32[2048]{0:T(1024)S(1)} %convert_reduce_fusion.2), channel_id=4, replica_groups=mesh['fsdp'=4,'ctx'=8] {'fsdp','ctx'}, use_global_device_ids=true, to_apply=%region_18.19.clone | all-reduce | flops 6144 | bytes 49152
  1268.2 29.4 %reduce-scatter.16.cloned.1.call-done = bf16[512,256]{1,0:T(8,128)(2,1)} async-done(((bf16[512,2048]{1,0:T(8,128)(2,1)}), bf16[512,256]{1,0:T(8,128)(2,1)}) %reduce-scatter.16.cloned.1.call-update) | async-done | bytes 262160 | tf_op jit(solution)/shard_map/reduce_scatter | solution.py:329
  1301.8 29.0 %reduce-scatter.10.cloned.1.call-done = bf16[128,2048]{1,0:T(8,128)(2,1)} async-done(((bf16[512,2048]{1,0:T(8,128)(2,1)}), bf16[128,2048]{1,0:T(8,128)(2,1)}) %reduce-scatter.10.cloned.1.call-update) | async-done | bytes 524304 | tf_op jit(solution)/shard_map/reduce_scatter | solution.py:193
  1332.9 120.0 %reduce-scatter.14.cloned.1.call-done = bf16[256,3,512]{2,0,1:T(8,128)(2,1)} async-done(((bf16[2048,3,512]{2,0,1:T(8,128)(2,1)}), bf16[256,3,512]{2,0,1:T(8,128)(2,1)}) %reduce-scatter.14.cloned.1.call-update) | async-done | bytes 786448 | tf_op jit(solution)/shard_map/reduce_scatter | solution.py:323
  1455.4 147.8 %reduce-scatter.18.cloned.1.call-done = bf16[256,2048]{1,0:T(8,128)(2,1)} async-done(((bf16[2048,2048]{1,0:T(8,128)(2,1)}), bf16[256,2048]{1,0:T(8,128)(2,1)}) %reduce-scatter.18.cloned.1.call-update) | async-done | bytes 1048592 | tf_op jit(solution)/shard_map/reduce_scatter | solution.py:332
  1605.9 147.7 %reduce-scatter.20.cloned.1.call-done = bf16[2048,256]{1,0:T(8,128)(2,1)} async-done(((bf16[2048,2048]{1,0:T(8,128)(2,1)}), bf16[2048,256]{1,0:T(8,128)(2,1)}) %reduce-scatter.20.cloned.1.call-update) | async-done | bytes 1048592 | tf_op jit(solution)/shard_map/reduce_scatter | solution.py:338
  (313 shorter events, 316.1 us)
Async XLA Ops:
  7.2 72.2 %all-gather.11.cloned.1.call-start = ((), (), s32[]{:S(2)}) async-start(), calls=%async_computation.7 | async-start | bytes 2621440 | tf_op jit(solution)/shard_map/all_gather | solution.py:102
  8.0 130.1 %all-gather.13.cloned.1.call-start = ((), (), s32[]{:S(2)}) async-start(), calls=%async_computation.8 | async-start | bytes 7077888 | tf_op jit(solution)/shard_map/all_gather | solution.py:106
  10.3 165.9 %all-gather.25.cloned.1.call-start = ((), (), s32[]{:S(2)}) async-start(), calls=%async_computation.15 | async-start | bytes 2621440 | tf_op jit(solution)/shard_map/all_gather | solution.py:103
  11.1 201.6 %all-gather.19.cloned.1.call-start = ((), (), s32[]{:S(2)}) async-start(), calls=%async_computation.11 | async-start | bytes 2359296 | tf_op jit(solution)/shard_map/all_gather | solution.py:107
  11.6 325.7 %all-gather.21.cloned.1.call-start = ((), (), s32[]{:S(2)}) async-start(), calls=%async_computation.12 | async-start | bytes 9437184 | tf_op jit(solution)/shard_map/all_gather | solution.py:108
  12.2 450.2 %all-gather.23.cloned.1.call-start = ((), (), s32[]{:S(2)}) async-start(), calls=%async_computation.13 | async-start | bytes 9437184 | tf_op jit(solution)/shard_map/all_gather | solution.py:109
  12.8 525.1 %all-gather.15.cloned.1.call-start = ((), (), s32[]{:S(2)}) async-start(), calls=%async_computation.9 | async-start | bytes 4718592 | tf_op jit(solution)/shard_map/all_gather | solution.py:148
  153.2 460.1 %all-gather.17.cloned.1.call-start = ((), (), s32[]{:S(2)}) async-start(), calls=%async_computation.10 | async-start | bytes 4718592 | tf_op jit(solution)/shard_map/all_gather | solution.py:149
  155.6 1058.4 %reduce-scatter.22.cloned.1.call-start = ((), (), s32[]{:S(2)}) async-start(), calls=%async_computation.21 | async-start | bytes 147456
  652.3 33.6 %collective-permute-start.1 = (bf16[2,4,128,512]{2,3,1,0:T(8,128)(2,1)}, bf16[2,4,128,512]{2,3,1,0:T(8,128)(2,1)S(1)}, u32[]{:S(2)}, u32[]{:S(2)}) collective-permute-start(bf16[2,4,128,512]{2,3,1,0:T(8,128)(2,1)} %convert_element_type.348), channel_id=1, source_target_pairs={{0,1},{1,2},{2,3},{3,4},{4,5},{5,6},{6,7},{7,0},{8,9},{9,10},{10,1... | collective-permute-start | bytes 3145736 | tf_op jit(solution)/shard_map/while/body/eval_jaxpr/ppermute | solution.py:26
  653.7 45.2 %collective-permute-start = (bf16[2,4,128,512]{2,3,1,0:T(8,128)(2,1)S(1)}, bf16[2,4,128,512]{2,3,1,0:T(8,128)(2,1)S(1)}, u32[]{:S(2)}, u32[]{:S(2)}) collective-permute-start(bf16[2,4,128,512]{2,3,1,0:T(8,128)(2,1)S(1)} %copy.171), channel_id=1, source_target_pairs={{0,1},{1,2},{2,3},{3,4},{4,5},{5,6},{6,7},{8,9},{9,10},{10,11},{11... | collective-permute-start | bytes 3145736 | tf_op jit(solution)/shard_map/while/body/eval_jaxpr/ppermute | solution.py:20
  702.0 43.8 %collective-permute-start.1 = (bf16[2,4,128,512]{2,3,1,0:T(8,128)(2,1)}, bf16[2,4,128,512]{2,3,1,0:T(8,128)(2,1)S(1)}, u32[]{:S(2)}, u32[]{:S(2)}) collective-permute-start(bf16[2,4,128,512]{2,3,1,0:T(8,128)(2,1)} %convert_element_type.348), channel_id=1, source_target_pairs={{0,1},{1,2},{2,3},{3,4},{4,5},{5,6},{6,7},{7,0},{8,9},{9,10},{10,1... | collective-permute-start | bytes 3145736 | tf_op jit(solution)/shard_map/while/body/eval_jaxpr/ppermute | solution.py:26
  714.6 44.3 %collective-permute-start = (bf16[2,4,128,512]{2,3,1,0:T(8,128)(2,1)S(1)}, bf16[2,4,128,512]{2,3,1,0:T(8,128)(2,1)S(1)}, u32[]{:S(2)}, u32[]{:S(2)}) collective-permute-start(bf16[2,4,128,512]{2,3,1,0:T(8,128)(2,1)S(1)} %copy.171), channel_id=1, source_target_pairs={{0,1},{1,2},{2,3},{3,4},{4,5},{5,6},{6,7},{8,9},{9,10},{10,11},{11... | collective-permute-start | bytes 3145736 | tf_op jit(solution)/shard_map/while/body/eval_jaxpr/ppermute | solution.py:20
  761.9 43.9 %collective-permute-start.1 = (bf16[2,4,128,512]{2,3,1,0:T(8,128)(2,1)}, bf16[2,4,128,512]{2,3,1,0:T(8,128)(2,1)S(1)}, u32[]{:S(2)}, u32[]{:S(2)}) collective-permute-start(bf16[2,4,128,512]{2,3,1,0:T(8,128)(2,1)} %convert_element_type.348), channel_id=1, source_target_pairs={{0,1},{1,2},{2,3},{3,4},{4,5},{5,6},{6,7},{7,0},{8,9},{9,10},{10,1... | collective-permute-start | bytes 3145736 | tf_op jit(solution)/shard_map/while/body/eval_jaxpr/ppermute | solution.py:26
  764.4 43.5 %collective-permute-start = (bf16[2,4,128,512]{2,3,1,0:T(8,128)(2,1)S(1)}, bf16[2,4,128,512]{2,3,1,0:T(8,128)(2,1)S(1)}, u32[]{:S(2)}, u32[]{:S(2)}) collective-permute-start(bf16[2,4,128,512]{2,3,1,0:T(8,128)(2,1)S(1)} %copy.171), channel_id=1, source_target_pairs={{0,1},{1,2},{2,3},{3,4},{4,5},{5,6},{6,7},{8,9},{9,10},{10,11},{11... | collective-permute-start | bytes 3145736 | tf_op jit(solution)/shard_map/while/body/eval_jaxpr/ppermute | solution.py:20
  810.9 54.0 %collective-permute-start.1 = (bf16[2,4,128,512]{2,3,1,0:T(8,128)(2,1)}, bf16[2,4,128,512]{2,3,1,0:T(8,128)(2,1)S(1)}, u32[]{:S(2)}, u32[]{:S(2)}) collective-permute-start(bf16[2,4,128,512]{2,3,1,0:T(8,128)(2,1)} %convert_element_type.348), channel_id=1, source_target_pairs={{0,1},{1,2},{2,3},{3,4},{4,5},{5,6},{6,7},{7,0},{8,9},{9,10},{10,1... | collective-permute-start | bytes 3145736 | tf_op jit(solution)/shard_map/while/body/eval_jaxpr/ppermute | solution.py:26
  825.9 41.8 %collective-permute-start = (bf16[2,4,128,512]{2,3,1,0:T(8,128)(2,1)S(1)}, bf16[2,4,128,512]{2,3,1,0:T(8,128)(2,1)S(1)}, u32[]{:S(2)}, u32[]{:S(2)}) collective-permute-start(bf16[2,4,128,512]{2,3,1,0:T(8,128)(2,1)S(1)} %copy.171), channel_id=1, source_target_pairs={{0,1},{1,2},{2,3},{3,4},{4,5},{5,6},{6,7},{8,9},{9,10},{10,11},{11... | collective-permute-start | bytes 3145736 | tf_op jit(solution)/shard_map/while/body/eval_jaxpr/ppermute | solution.py:20
  870.7 52.4 %collective-permute-start.1 = (bf16[2,4,128,512]{2,3,1,0:T(8,128)(2,1)}, bf16[2,4,128,512]{2,3,1,0:T(8,128)(2,1)S(1)}, u32[]{:S(2)}, u32[]{:S(2)}) collective-permute-start(bf16[2,4,128,512]{2,3,1,0:T(8,128)(2,1)} %convert_element_type.348), channel_id=1, source_target_pairs={{0,1},{1,2},{2,3},{3,4},{4,5},{5,6},{6,7},{7,0},{8,9},{9,10},{10,1... | collective-permute-start | bytes 3145736 | tf_op jit(solution)/shard_map/while/body/eval_jaxpr/ppermute | solution.py:26
  874.1 50.5 %collective-permute-start = (bf16[2,4,128,512]{2,3,1,0:T(8,128)(2,1)S(1)}, bf16[2,4,128,512]{2,3,1,0:T(8,128)(2,1)S(1)}, u32[]{:S(2)}, u32[]{:S(2)}) collective-permute-start(bf16[2,4,128,512]{2,3,1,0:T(8,128)(2,1)S(1)} %copy.171), channel_id=1, source_target_pairs={{0,1},{1,2},{2,3},{3,4},{4,5},{5,6},{6,7},{8,9},{9,10},{10,11},{11... | collective-permute-start | bytes 3145736 | tf_op jit(solution)/shard_map/while/body/eval_jaxpr/ppermute | solution.py:20
  927.6 52.9 %collective-permute-start.1 = (bf16[2,4,128,512]{2,3,1,0:T(8,128)(2,1)}, bf16[2,4,128,512]{2,3,1,0:T(8,128)(2,1)S(1)}, u32[]{:S(2)}, u32[]{:S(2)}) collective-permute-start(bf16[2,4,128,512]{2,3,1,0:T(8,128)(2,1)} %convert_element_type.348), channel_id=1, source_target_pairs={{0,1},{1,2},{2,3},{3,4},{4,5},{5,6},{6,7},{7,0},{8,9},{9,10},{10,1... | collective-permute-start | bytes 3145736 | tf_op jit(solution)/shard_map/while/body/eval_jaxpr/ppermute | solution.py:26
  931.6 50.5 %collective-permute-start = (bf16[2,4,128,512]{2,3,1,0:T(8,128)(2,1)S(1)}, bf16[2,4,128,512]{2,3,1,0:T(8,128)(2,1)S(1)}, u32[]{:S(2)}, u32[]{:S(2)}) collective-permute-start(bf16[2,4,128,512]{2,3,1,0:T(8,128)(2,1)S(1)} %copy.171), channel_id=1, source_target_pairs={{0,1},{1,2},{2,3},{3,4},{4,5},{5,6},{6,7},{8,9},{9,10},{10,11},{11... | collective-permute-start | bytes 3145736 | tf_op jit(solution)/shard_map/while/body/eval_jaxpr/ppermute | solution.py:20
  985.0 52.1 %collective-permute-start.1 = (bf16[2,4,128,512]{2,3,1,0:T(8,128)(2,1)}, bf16[2,4,128,512]{2,3,1,0:T(8,128)(2,1)S(1)}, u32[]{:S(2)}, u32[]{:S(2)}) collective-permute-start(bf16[2,4,128,512]{2,3,1,0:T(8,128)(2,1)} %convert_element_type.348), channel_id=1, source_target_pairs={{0,1},{1,2},{2,3},{3,4},{4,5},{5,6},{6,7},{7,0},{8,9},{9,10},{10,1... | collective-permute-start | bytes 3145736 | tf_op jit(solution)/shard_map/while/body/eval_jaxpr/ppermute | solution.py:26
  985.0 53.5 %collective-permute-start = (bf16[2,4,128,512]{2,3,1,0:T(8,128)(2,1)S(1)}, bf16[2,4,128,512]{2,3,1,0:T(8,128)(2,1)S(1)}, u32[]{:S(2)}, u32[]{:S(2)}) collective-permute-start(bf16[2,4,128,512]{2,3,1,0:T(8,128)(2,1)S(1)} %copy.171), channel_id=1, source_target_pairs={{0,1},{1,2},{2,3},{3,4},{4,5},{5,6},{6,7},{8,9},{9,10},{10,11},{11... | collective-permute-start | bytes 3145736 | tf_op jit(solution)/shard_map/while/body/eval_jaxpr/ppermute | solution.py:20
  1041.6 51.2 %collective-permute-start.1 = (bf16[2,4,128,512]{2,3,1,0:T(8,128)(2,1)}, bf16[2,4,128,512]{2,3,1,0:T(8,128)(2,1)S(1)}, u32[]{:S(2)}, u32[]{:S(2)}) collective-permute-start(bf16[2,4,128,512]{2,3,1,0:T(8,128)(2,1)} %convert_element_type.348), channel_id=1, source_target_pairs={{0,1},{1,2},{2,3},{3,4},{4,5},{5,6},{6,7},{7,0},{8,9},{9,10},{10,1... | collective-permute-start | bytes 3145736 | tf_op jit(solution)/shard_map/while/body/eval_jaxpr/ppermute | solution.py:26
  1041.6 52.7 %collective-permute-start = (bf16[2,4,128,512]{2,3,1,0:T(8,128)(2,1)S(1)}, bf16[2,4,128,512]{2,3,1,0:T(8,128)(2,1)S(1)}, u32[]{:S(2)}, u32[]{:S(2)}) collective-permute-start(bf16[2,4,128,512]{2,3,1,0:T(8,128)(2,1)S(1)} %copy.171), channel_id=1, source_target_pairs={{0,1},{1,2},{2,3},{3,4},{4,5},{5,6},{6,7},{8,9},{9,10},{10,11},{11... | collective-permute-start | bytes 3145736 | tf_op jit(solution)/shard_map/while/body/eval_jaxpr/ppermute | solution.py:20
  1110.5 114.1 %reduce-scatter.12.cloned.1.call-start = ((), (), s32[]{:S(2)}) async-start(), calls=%async_computation.16 | async-start | bytes 2621440 | tf_op jit(solution)/shard_map/reduce_scatter | solution.py:300
  1126.1 171.4 %reduce-scatter.16.cloned.1.call-start = ((), (), s32[]{:S(2)}) async-start(), calls=%async_computation.18 | async-start | bytes 2359296 | tf_op jit(solution)/shard_map/reduce_scatter | solution.py:329
  1128.8 202.0 %reduce-scatter.10.cloned.1.call-start = ((), (), s32[]{:S(2)}) async-start(), calls=%async_computation.14 | async-start | bytes 2621440 | tf_op jit(solution)/shard_map/reduce_scatter | solution.py:193
  1140.8 312.1 %reduce-scatter.14.cloned.1.call-start = ((), (), s32[]{:S(2)}) async-start(), calls=%async_computation.17 | async-start | bytes 7077888 | tf_op jit(solution)/shard_map/reduce_scatter | solution.py:323
  1147.7 455.5 %reduce-scatter.18.cloned.1.call-start = ((), (), s32[]{:S(2)}) async-start(), calls=%async_computation.19 | async-start | bytes 9437184 | tf_op jit(solution)/shard_map/reduce_scatter | solution.py:332
  1159.2 594.5 %reduce-scatter.20.cloned.1.call-start = ((), (), s32[]{:S(2)}) async-start(), calls=%async_computation.20 | async-start | bytes 9437184 | tf_op jit(solution)/shard_map/reduce_scatter | solution.py:338
  1267.0 489.3 %copy-start.36 = (f32[64]{0:T(128)}, f32[64]{0:T(128)S(1)}, u32[]{:S(2)}) copy-start(f32[64]{0:T(128)S(1)} %dynamic-slice.2) | copy-start | bytes 772
  (38 other events, 1382.4 us)
Sparse Core Ops, SparseCore 0:
  9.6 25.9 all-gather.10
  38.2 99.8 all-gather.12
  139.7 20.7 all-gather.24
  162.3 50.3 all-gather.18
  214.7 122.6 all-gather.20
  339.3 123.1 all-gather.22
  465.0 72.8 all-gather.14
  540.5 72.8 all-gather.16
  1110.6 81.3 reduce-scatter.21
  1194.4 30.1 reduce-scatter.11
  1228.1 69.3 reduce-scatter.15
  1300.5 30.2 reduce-scatter.9
  1334.4 118.4 reduce-scatter.13
  1456.4 146.7 reduce-scatter.17
  1606.6 146.9 reduce-scatter.19
where the time goes:
time: 1770 us; the launch traced here: 1760 us
  waiting for transfers between devices  1240 us (70%)
  blocking collectives  163 us (9%)
  matrix products  108 us (6%)
  starting transfers between devices  98.5 us (6%)
  other arithmetic  72.2 us (4%)
  local copies, waits for them, and re-layouts  68.2 us (4%)
    ppermute x8, waiting for transfers between devices, passed_along_2(): return lax.ppermute(value, axis, pairs)  286 us
    reduce_scatter x1, waiting for transfers between devices, body(): lax.psum_scatter(grad_fc1_w.astype(jnp.bfloat16), 'ctx', scatter_dimensio...  148 us
    reduce_scatter x1, waiting for transfers between devices, body(): lax.psum_scatter(grad_fc2_w.astype(jnp.bfloat16), 'ctx', scatter_dimensio...  148 us
    unnamed x3, blocking collectives  124 us
    reduce_scatter x1, waiting for transfers between devices, body(): lax.psum_scatter(grad_qkv_w.astype(jnp.bfloat16), 'ctx', scatter_dimensio...  120 us
    all_gather x1, waiting for transfers between devices, body(): lax.all_gather(fc2_weight, 'ctx', axis=1, tiled=True)  114 us
    all_gather x1, waiting for transfers between devices, body(): lax.all_gather(fc1_weight, 'ctx', axis=0, tiled=True)  113 us
    all_gather x1, waiting for transfers between devices, body(): value_piece = lax.all_gather(value_flat, 'ctx', axis=1, tiled=True)  62.3 us
  transfers between devices with their start and end apart: 31, of which 24 were waited for; matrix products, arithmetic and copies ran while one was open for 10% of the time, Pallas kernels for 0%

commit v1 on v0

v1 whole, which is shorter than its diff:
```python
import functools
import math

import jax
import jax.numpy as jnp
from jax import lax
from jax.experimental import pallas as pl
from jax.experimental.pallas import tpu as pltpu
from jax.sharding import PartitionSpec as P

HEAD_DIM = 64
ROT_DIM = 32
NORM_EPS = 1e-05
GELU_COEF = math.sqrt(2.0 / math.pi)
MASKED = -1e30
LOW = 2
F32 = jnp.float32
BF16 = jnp.bfloat16
ANY = pl.BlockSpec(memory_space=pl.ANY)
VMEM = pl.BlockSpec(memory_space=pltpu.VMEM)


class Axis:
    def __init__(self, name, size):
        self.name = name
        self.size = size
        self.low = LOW
        self.high = size // LOW
        self.me = lax.axis_index(name)
        self.hi = lax.div(self.me, LOW)
        self.lo = lax.rem(self.me, LOW)
        self.partner = self.hi * LOW + (1 - self.lo)

    def at(self, hi, lo):
        return hi * LOW + lo

    def ahead(self, steps):
        return self.at(lax.rem(self.hi + steps, self.high), self.lo)

    def behind(self, steps):
        return self.at(lax.rem(self.hi + self.high - steps, self.high), self.lo)

    def behind_other(self, steps):
        return self.at(lax.rem(self.hi + self.high - steps, self.high), 1 - self.lo)


def remote(src, dst, send_sem, recv_sem, axis, index):
    return pltpu.make_async_remote_copy(
        src_ref=src,
        dst_ref=dst,
        send_sem=send_sem,
        recv_sem=recv_sem,
        device_id={axis.name: index},
        device_id_type=pl.DeviceIdType.MESH,
    )


def arrived(dst, sem):
    pltpu.make_async_copy(dst, dst, sem).wait()


class Spread:
    def __init__(self, axis, slot, source, send_hi, recv_hi, send_lo, recv_lo):
        self.axis, self.slot, self.source = axis, slot, source
        self.send_hi, self.recv_hi, self.send_lo, self.recv_lo = send_hi, recv_hi, send_lo, recv_lo

    def copy_hi(self, step):
        ax = self.axis
        return remote(
            self.source,
            self.slot(ax.me),
            self.send_hi.at[step - 1],
            self.recv_hi.at[step - 1],
            ax,
            ax.ahead(step),
        )

    def copy_lo(self, step):
        ax = self.axis
        held = ax.behind(step)
        src = self.source if step == 0 else self.slot(held)
        return remote(
            src, self.slot(held), self.send_lo.at[step], self.recv_lo.at[step], ax, ax.partner
        )

    def start(self):
        for step in range(1, self.axis.high):
            self.copy_hi(step).start()
        self.copy_lo(0).start()

    def forward(self, step):
        arrived(self.slot(self.axis.behind(step)), self.recv_hi.at[step - 1])
        self.copy_lo(step).start()

    def finish(self):
        for step in range(self.axis.high):
            arrived(self.slot(self.axis.behind_other(step)), self.recv_lo.at[step])
        for step in range(1, self.axis.high):
            self.copy_hi(step).wait_send()
        for step in range(self.axis.high):
            self.copy_lo(step).wait_send()


def spread_sems(axis_size):
    high = axis_size // LOW
    return [
        pltpu.SemaphoreType.DMA((max(high - 1, 1),)),
        pltpu.SemaphoreType.DMA((max(high - 1, 1),)),
        pltpu.SemaphoreType.DMA((high,)),
        pltpu.SemaphoreType.DMA((high,)),
    ]


class Line:
    def __init__(self, axis, slot, source, *sems):
        self.axis, self.slot, self.source = axis, slot, source
        self.send_up, self.recv_up, self.send_down, self.recv_down, self.send_lo, self.recv_lo = (
            sems
        )

    def copy(self, hi, sends, recvs, target):
        ax = self.axis
        block = ax.at(hi, ax.lo)
        src = self.source if hi is ax.hi else self.slot(block)
        return remote(src, self.slot(block), sends.at[hi], recvs.at[hi], ax, target)

    def up(self, hi):
        return self.copy(hi, self.send_up, self.recv_up, self.axis.me + LOW)

    def down(self, hi):
        return self.copy(hi, self.send_down, self.recv_down, self.axis.me - LOW)

    def across(self, hi):
        return self.copy(hi, self.send_lo, self.recv_lo, self.axis.partner)

    def start(self):
        ax = self.axis

        @pl.when(ax.hi < ax.high - 1)
        def _():
            self.up(ax.hi).start()

        @pl.when(ax.hi > 0)
        def _():
            self.down(ax.hi).start()

        self.across(ax.hi).start()

    def forward(self, step):
        ax = self.axis

        @pl.when(ax.hi >= step)
        def _():
            held = ax.hi - step
            arrived(self.slot(ax.at(held, ax.lo)), self.recv_up.at[held])

            @pl.when(ax.hi < ax.high - 1)
            def _():
                self.up(held).start()

            self.across(held).start()

        @pl.when(ax.hi + step < ax.high)
        def _():
            held = ax.hi + step
            arrived(self.slot(ax.at(held, ax.lo)), self.recv_down.at[held])

            @pl.when(ax.hi > 0)
            def _():
                self.down(held).start()

            self.across(held).start()

    def finish(self):
        ax = self.axis
        for hi in range(ax.high):
            arrived(self.slot(ax.at(hi, 1 - ax.lo)), self.recv_lo.at[hi])
        for step in range(ax.high):

            @pl.when(jnp.logical_and(ax.hi >= step, ax.hi < ax.high - 1))
            def _(step=step):
                self.up(ax.hi if step == 0 else ax.hi - step).wait_send()

            @pl.when(jnp.logical_and(ax.hi + step < ax.high, ax.hi > 0))
            def _(step=step):
                self.down(ax.hi if step == 0 else ax.hi + step).wait_send()

            @pl.when(ax.hi >= step)
            def _(step=step):
                self.across(ax.hi if step == 0 else ax.hi - step).wait_send()

            if step > 0:

                @pl.when(ax.hi + step < ax.high)
                def _(step=step):
                    self.across(ax.hi + step).wait_send()


def line_sems(axis_size):
    return [pltpu.SemaphoreType.DMA((axis_size // LOW,))] * 6


def meet_everyone(fs, cx):
    barrier = pltpu.get_barrier_semaphore()
    total = fs.size * cx.size
    me = fs.me * cx.size + cx.me

    def signal(step, carry):
        other = lax.rem(me + step, total)
        pl.semaphore_signal(
            barrier,
            inc=1,
            device_id={fs.name: lax.div(other, cx.size), cx.name: lax.rem(other, cx.size)},
            device_id_type=pl.DeviceIdType.MESH,
        )
        return carry

    lax.fori_loop(1, total, signal, 0)
    pl.semaphore_wait(barrier, total - 1)


def shift_of(f_index, f_size):
    return lax.rem(f_index, LOW) * (f_size // LOW) + lax.div(f_index, LOW)


def unshift(shift, f_size):
    return lax.rem(shift, f_size // LOW) * LOW + lax.div(shift, f_size // LOW)


def low_slot(fs, column, device):
    return lax.rem(device + fs.size - shift_of(column, fs.size), fs.size)


def gather_kernel(n_act, n_w, small, f_size, c_size, *refs):
    fs, cx = Axis("fsdp", f_size), Axis("ctx", c_size)
    ratio = c_size // f_size
    n_ctx = n_act + (1 if small else 0)
    n_in = n_ctx + n_w
    ins, outs, rest = refs[:n_in], refs[n_in : 2 * n_in], list(refs[2 * n_in :])
    acts, w_srcs = ins[:n_ctx], ins[n_ctx:]
    act_outs, w_outs = outs[:n_ctx], outs[n_ctx:]
    own_sem = rest.pop(0)
    lines = []
    for index in range(n_ctx):
        out = act_outs[index]
        if index < n_act:
            slot = lambda c, out=out: out.at[c]
        else:
            slot = lambda c, out=out: out.at[fs.me, c]
        lines.append(Line(cx, slot, acts[index], *rest[:6]))
        rest = rest[6:]
    mids, rest = rest[:n_w], rest[n_w:]
    mid_send, mid_recv, w_send, w_recv = rest[:4]
    rest = rest[4:]
    column = lax.div(cx.me, ratio)
    spreads = []
    for index in range(n_w):
        out = w_outs[index]
        slot = lambda f, out=out: out.at[:, low_slot(fs, column, f)]
        spreads.append(Spread(fs, slot, slot(fs.me), *rest[:4]))
        rest = rest[4:]
    if small:
        out = act_outs[n_act]
        slot = lambda f, out=out: out.at[f]
        small_spread = Spread(fs, slot, slot(fs.me), *rest[:4])

    pass_to = lax.rem(cx.me + shift_of(fs.me, f_size), f_size)
    pass_from = unshift(lax.rem(fs.me + f_size - lax.rem(cx.me, f_size), f_size), f_size)
    stays = pass_to == fs.me
    row_hi, row_lo = lax.div(cx.me, f_size), lax.rem(cx.me, f_size)

    def move(index):
        src, dst = w_srcs[index], mids[index]
        away = lambda: remote(src, dst, mid_send.at[index], mid_recv.at[index], fs, pass_to)
        here = lambda: pltpu.make_async_copy(src, dst, mid_recv.at[index])
        return away, here

    def scatter(index, i):
        to_c = pass_from * ratio + i
        src, dst = mids[index].at[i], w_outs[index].at[row_hi, row_lo]
        sem = w_recv.at[index, row_hi]
        away = lambda: remote(src, dst, w_send.at[index, i], sem, cx, to_c)
        here = lambda: pltpu.make_async_copy(src, dst, sem)
        return to_c == cx.me, away, here

    def either(is_self, away, here):
        @pl.when(is_self)
        def _():
            here().start()

        @pl.when(jnp.logical_not(is_self))
        def _():
            away().start()

    def start_moves():
        for index in range(n_w):
            either(stays, *move(index))

    def start_scatter(index):
        arrived(mids[index], mid_recv.at[index])
        for i in range(ratio):
            either(*scatter(index, i))

    def start_spread(index):
        for hi in range(ratio):
            arrived(w_outs[index].at[hi, low_slot(fs, column, fs.me)], w_recv.at[index, hi])
        spreads[index].start()

    def forward_spread(index):
        for step in range(1, fs.high):
            spreads[index].forward(step)

    meet_everyone(fs, cx)
    own = []
    for index in range(n_ctx):
        copy = pltpu.make_async_copy(acts[index], lines[index].slot(cx.me), own_sem.at[index])
        copy.start()
        own.append(copy)
    if small:
        lines[n_act].start()
    start_moves()
    for index in range(n_act):
        lines[index].start()
    scatters = [functools.partial(start_scatter, index) for index in range(n_w)]
    starts = [functools.partial(start_spread, index) for index in range(n_w)]
    lasts = [functools.partial(forward_spread, index) for index in range(n_w)]
    for work in scatters[:2]:
        work()
    for step in range(1, cx.high):
        if small:
            lines[n_act].forward(step)
        for index in range(n_act):
            lines[index].forward(step)
            if step == 1 and index == n_act - 1:
                for work in scatters[2:]:
                    work()
            if starts and (step > 1 or index == n_act - 1):
                starts.pop(0)()
                if len(lasts) - len(starts) > 1:
                    lasts.pop(0)()
    for work in scatters[2:] if cx.high == 1 else []:
        work()
    while starts:
        starts.pop(0)()
        if len(lasts) - len(starts) > 1:
            lasts.pop(0)()
    for work in lasts:
        work()
    if small:
        lines[n_act].finish()
        own[n_act].wait()
        small_spread.start()
        for step in range(1, fs.high):
            small_spread.forward(step)
    for index in range(n_act):
        own[index].wait()
        lines[index].finish()
    for index in range(n_w):
        spreads[index].finish()

        @pl.when(jnp.logical_not(stays))
        def _(index=index):
            move(index)[0]().wait_send()

        for i in range(ratio):
            is_self, away, here = scatter(index, i)

            @pl.when(jnp.logical_not(is_self))
            def _(away=away):
                away().wait_send()

    if small:
        small_spread.finish()


def gather_call(f_size, c_size, acts, w_srcs, small, collective_id):
    ratio = c_size // f_size
    ins = list(acts) + ([small] if small is not None else []) + list(w_srcs)
    shapes = [jax.ShapeDtypeStruct((c_size, *a.shape), a.dtype) for a in acts]
    if small is not None:
        shapes.append(jax.ShapeDtypeStruct((f_size, c_size, *small.shape), small.dtype))
    for w in w_srcs:
        shapes.append(jax.ShapeDtypeStruct((ratio, f_size, *w.shape[1:]), w.dtype))
    n_ctx = len(acts) + (small is not None)
    scratch = [pltpu.SemaphoreType.DMA((n_ctx,))]
    for _ in range(n_ctx):
        scratch += line_sems(c_size)
    scratch += [pltpu.VMEM(w.shape, w.dtype) for w in w_srcs]
    scratch += [pltpu.SemaphoreType.DMA((len(w_srcs),))] * 2
    scratch += [pltpu.SemaphoreType.DMA((len(w_srcs), ratio))] * 2
    for _ in range(len(w_srcs) + (small is not None)):
        scratch += spread_sems(f_size)
    return pl.pallas_call(
        functools.partial(
            gather_kernel, len(acts), len(w_srcs), small is not None, f_size, c_size
        ),
        out_shape=tuple(shapes),
        in_specs=[VMEM] * len(ins),
        out_specs=tuple([ANY] * len(shapes)),
        scratch_shapes=scratch,
        compiler_params=pltpu.CompilerParams(collective_id=collective_id, has_side_effects=True),
        name=f"gather_{collective_id}",
    )(*ins)


def add_into(dst, terms):
    rows = dst.shape[-2]
    lead = dst.shape[:-2]
    chunk = math.gcd(rows, 32)

    def at(ref, index, start):
        return (*index, pl.ds(start, chunk), slice(None))

    for index in [()] if not lead else [(i,) for i in range(lead[0])]:

        def step(i, carry, index=index):
            start = pl.multiple_of(i * chunk, chunk)
            total = terms[0][at(terms[0], index, start)].astype(F32)
            for term in terms[1:]:
                total = total + term[at(term, index, start)].astype(F32)
            dst[at(dst, index, start)] = total.astype(dst.dtype)
            return carry

        lax.fori_loop(0, rows // chunk, step, 0)


class Fold:
    def __init__(self, axis, block, result, from_lo, staged, from_hi, sems):
        self.axis, self.block, self.result = axis, block, result
        self.from_lo, self.staged, self.from_hi = from_lo, staged, from_hi
        self.send_lo, self.recv_lo, self.send_hi, self.recv_hi = sems

    def copy_lo(self, step):
        ax = self.axis
        hi = lax.rem(ax.hi + step, ax.high)
        return remote(
            self.block(ax.at(hi, 1 - ax.lo)),
            self.from_lo.at[step],
            self.send_lo.at[step],
            self.recv_lo.at[step],
            ax,
            ax.partner,
        )

    def copy_hi(self, step):
        ax = self.axis
        return remote(
            self.staged.at[step - 1],
            self.from_hi.at[step - 1],
            self.send_hi.at[step - 1],
            self.recv_hi.at[step - 1],
            ax,
            ax.ahead(step),
        )

    def start(self):
        for step in list(range(1, self.axis.high)) + [0]:
            self.copy_lo(step).start()

    def forward(self, step):
        arrived(self.from_lo.at[step], self.recv_lo.at[step])
        add_into(
            self.staged.at[step - 1], [self.block(self.axis.ahead(step)), self.from_lo.at[step]]
        )
        self.copy_hi(step).start()

    def finish(self):
        arrived(self.from_lo.at[0], self.recv_lo.at[0])
        terms = [self.block(self.axis.me), self.from_lo.at[0]]
        for step in range(1, self.axis.high):
            arrived(self.from_hi.at[step - 1], self.recv_hi.at[step - 1])
            terms.append(self.from_hi.at[step - 1])
        add_into(self.result, terms)

    def drain(self):
        for step in range(self.axis.high):
            self.copy_lo(step).wait_send()
        for step in range(1, self.axis.high):
            self.copy_hi(step).wait_send()


class LineFold:
    def __init__(self, axis, block, result, from_lo, from_z, from_end, *sems):
        self.axis, self.block, self.result = axis, block, result
        self.from_lo, self.from_z, self.from_end = from_lo, from_z, from_end
        self.send_lo, self.recv_lo, self.send_z, self.recv_z, self.recv_end = sems
        low_end, high_end = jnp.int32(0), jnp.int32(axis.high - 1)
        self.order = []
        for _ in range(axis.high):
            take_low = axis.hi - low_end >= high_end - axis.hi
            self.order.append(jnp.where(take_low, low_end, high_end))
            low_end = jnp.where(take_low, low_end + 1, low_end)
            high_end = jnp.where(take_low, high_end, high_end - 1)

    def across(self, hi):
        ax = self.axis
        return remote(
            self.block(ax.at(hi, 1 - ax.lo)),
            self.from_lo.at[hi],
            self.send_lo.at[hi],
            self.recv_lo.at[hi],
            ax,
            ax.partner,
        )

    def onward(self, hi, up, last):
        ax = self.axis
        side = 0 if up else 1
        dst, sem = (
            (self.from_end.at[side], self.recv_end.at[side])
            if last
            else (self.from_z.at[hi], self.recv_z.at[hi])
        )
        target = ax.me + LOW if up else ax.me - LOW
        return remote(self.from_lo.at[hi], dst, self.send_z.at[hi], sem, ax, target)

    def start(self):
        for hi in self.order:
            self.across(hi).start()

    def pass_on(self, hi, up):
        ax = self.axis
        first = ax.hi == (0 if up else ax.high - 1)
        own = self.block(ax.at(hi, ax.lo))

        @pl.when(first)
        def _():
            add_into(self.from_lo.at[hi], [own, self.from_lo.at[hi]])

        @pl.when(jnp.logical_not(first))
        def _():
            arrived(self.from_z.at[hi], self.recv_z.at[hi])
            add_into(self.from_lo.at[hi], [own, self.from_lo.at[hi], self.from_z.at[hi]])

        near = ax.hi == (hi - 1 if up else hi + 1)

        @pl.when(near)
        def _():
            self.onward(hi, up, True).start()

        @pl.when(jnp.logical_not(near))
        def _():
            self.onward(hi, up, False).start()

    def forward(self, hi):
        ax = self.axis
        arrived(self.from_lo.at[hi], self.recv_lo.at[hi])

        @pl.when(ax.hi < hi)
        def _():
            self.pass_on(hi, True)

        @pl.when(ax.hi > hi)
        def _():
            self.pass_on(hi, False)

    def finish(self):
        ax = self.axis
        own = [self.block(ax.me), self.from_lo.at[ax.hi]]
        if ax.high == 1:
            add_into(self.result, own)
            return
        low_end, high_end = ax.hi == 0, ax.hi == ax.high - 1

        @pl.when(jnp.logical_not(low_end))
        def _():
            arrived(self.from_end.at[0], self.recv_end.at[0])

        @pl.when(jnp.logical_not(high_end))
        def _():
            arrived(self.from_end.at[1], self.recv_end.at[1])

        @pl.when(low_end)
        def _():
            add_into(self.result, own + [self.from_end.at[1]])

        @pl.when(high_end)
        def _():
            add_into(self.result, own + [self.from_end.at[0]])

        @pl.when(jnp.logical_not(jnp.logical_or(low_end, high_end)))
        def _():
            add_into(self.result, own + [self.from_end.at[0], self.from_end.at[1]])

    def drain(self):
        ax = self.axis
        for hi in range(ax.high):
            self.across(hi).wait_send()

            @pl.when(ax.hi != hi)
            def _(hi=hi):
                self.onward(hi, True, False).wait_send()


def line_fold_scratch(axis_size, shape, dtype):
    high = axis_size // LOW
    return [
        pltpu.VMEM((high, *shape), dtype),
        pltpu.VMEM((high, *shape), dtype),
        pltpu.VMEM((2, *shape), dtype),
        pltpu.SemaphoreType.DMA((high,)),
        pltpu.SemaphoreType.DMA((high,)),
        pltpu.SemaphoreType.DMA((high,)),
        pltpu.SemaphoreType.DMA((high,)),
        pltpu.SemaphoreType.DMA((2,)),
    ]


def fold_scratch(axis_size, shape, dtype):
    high = axis_size // LOW
    more = max(high - 1, 1)
    return [
        pltpu.VMEM((high, *shape), dtype),
        pltpu.VMEM((more, *shape), dtype),
        pltpu.VMEM((more, *shape), dtype),
        pltpu.SemaphoreType.DMA((high,)),
        pltpu.SemaphoreType.DMA((high,)),
        pltpu.SemaphoreType.DMA((more,)),
        pltpu.SemaphoreType.DMA((more,)),
    ]


def reduce_kernel(n_part, n_w, f_size, c_size, *refs):
    fs, cx = Axis("fsdp", f_size), Axis("ctx", c_size)
    ratio = c_size // f_size
    parts, refs = refs[:n_part], refs[n_part:]
    grads, refs = refs[:n_w], refs[n_w:]
    rows_outs, refs = refs[:n_part], refs[n_part:]
    grad_outs, scratch = refs[:n_w], list(refs[n_w:])
    row_folds = []
    for index in range(n_part):
        block = lambda c, part=parts[index]: part.at[c]
        row_folds.append(LineFold(cx, block, rows_outs[index], *scratch[:8]))
        scratch = scratch[8:]
    column = lax.div(cx.me, ratio)
    folds, totals = [], []
    for index in range(n_w):
        grad = grads[index]
        block = lambda f, grad=grad: grad.at[:, low_slot(fs, column, f)]
        totals.append(scratch[7])
        folds.append(Fold(fs, block, scratch[7], *scratch[:3], scratch[3:7]))
        scratch = scratch[8:]
    g_send, g_recv = scratch

    meet_everyone(fs, cx)
    for fold in row_folds:
        fold.start()
    for fold in folds:
        fold.start()

    slot = lax.rem(cx.me, ratio)
    row_lo = low_slot(fs, column, fs.me)

    def deliver(index, hi):
        to_c = hi * f_size + row_lo
        is_self = jnp.logical_and(column == fs.me, to_c == cx.me)
        src = totals[index].at[hi]
        dst = grad_outs[index].at[slot]
        away = lambda: pltpu.make_async_remote_copy(
            src_ref=src,
            dst_ref=dst,
            send_sem=g_send.at[index, hi],
            recv_sem=g_recv.at[index, slot],
            device_id={fs.name: column, cx.name: to_c},
            device_id_type=pl.DeviceIdType.MESH,
        )
        here = lambda: pltpu.make_async_copy(src, dst, g_recv.at[index, slot])
        return is_self, away, here

    def deliver_all(index):
        folds[index].finish()
        for hi in range(ratio):
            is_self, away, here = deliver(index, hi)

            @pl.when(is_self)
            def _(here=here):
                here().start()

            @pl.when(jnp.logical_not(is_self))
            def _(away=away):
                away().start()

    def pass_halves(index):
        for step in range(1, fs.high):
            folds[index].forward(step)

    row_work = [
        functools.partial(fold.forward, hi) for fold in row_folds for hi in fold.order
    ]
    halves = [functools.partial(pass_halves, index) for index in range(n_w)]
    delivers = [functools.partial(deliver_all, index) for index in range(n_w)]
    for count, work in enumerate(row_work):
        for more in halves[:2]:
            more()
        halves = halves[2:]
        work()
        if count >= 1 and delivers and not halves:
            delivers.pop(0)()
    for work in halves + delivers:
        work()
    for fold in row_folds:
        fold.finish()
    for index in range(n_w):
        for i in range(ratio):
            arrived(grad_outs[index].at[i], g_recv.at[index, i])
    for fold in row_folds:
        fold.drain()
    for index in range(n_w):
        folds[index].drain()
        for hi in range(ratio):
            is_self, away, here = deliver(index, hi)

            @pl.when(jnp.logical_not(is_self))
            def _(away=away):
                away().wait_send()


def reduce_call(f_size, c_size, parts, grads, collective_id):
    ratio = c_size // f_size
    shapes, scratch = [], []
    for part in parts:
        shapes.append(jax.ShapeDtypeStruct(part.shape[1:], F32))
        scratch += line_fold_scratch(c_size, part.shape[1:], part.dtype)
    for g in grads:
        piece = (ratio, *g.shape[2:])
        shapes.append(jax.ShapeDtypeStruct(piece, g.dtype))
        scratch += fold_scratch(f_size, piece, g.dtype) + [pltpu.VMEM(piece, g.dtype)]
    scratch += [pltpu.SemaphoreType.DMA((len(grads), ratio))] * 2
    outs = pl.pallas_call(
        functools.partial(reduce_kernel, len(parts), len(grads), f_size, c_size),
        out_shape=tuple(shapes),
        in_specs=[VMEM] * (len(parts) + len(grads)),
        out_specs=tuple([VMEM] * len(shapes)),
        scratch_shapes=scratch,
        compiler_params=pltpu.CompilerParams(collective_id=collective_id, has_side_effects=True),
        name=f"reduce_{collective_id}",
    )(*parts, *grads)
    return outs[: len(parts)], outs[len(parts) :]


def reduce_all(f_size, c_size, parts, grads):
    size = sum(2.25 * part.size * part.dtype.itemsize for part in parts)
    size += sum(2.5 * grad.size * grad.dtype.itemsize for grad in grads)
    if size <= 56 * 2**20:
        return reduce_call(f_size, c_size, parts, grads, 2)
    half = len(grads) // 2
    (first,), early = reduce_call(f_size, c_size, parts[:1], grads[:half], 2)
    (second,), late = reduce_call(f_size, c_size, parts[1:], grads[half:], 3)
    return (first, second), (*early, *late)


def small_kernel(f_size, c_size, tiles, out, held, send_sem, recv_sem):
    fs, cx = Axis("fsdp", f_size), Axis("ctx", c_size)
    total = f_size * c_size
    me = fs.me * c_size + cx.me
    meet_everyone(fs, cx)

    def copy(step):
        other = lax.rem(me + step, total)
        return pltpu.make_async_remote_copy(
            src_ref=tiles.at[other],
            dst_ref=held.at[step - 1],
            send_sem=send_sem.at[step - 1],
            recv_sem=recv_sem.at[step - 1],
            device_id={fs.name: lax.div(other, c_size), cx.name: lax.rem(other, c_size)},
            device_id_type=pl.DeviceIdType.MESH,
        )

    def start(step, carry):
        copy(step).start()
        return carry

    lax.fori_loop(1, total, start, 0)

    def collect(step, acc):
        arrived(held.at[step - 1], recv_sem.at[step - 1])
        return acc + held[step - 1]

    out[...] = lax.fori_loop(1, total, collect, tiles[me])

    def drain(step, carry):
        copy(step).wait_send()
        return carry

    lax.fori_loop(1, total, drain, 0)


def small_call(f_size, c_size, tiles, collective_id):
    total = f_size * c_size
    return pl.pallas_call(
        functools.partial(small_kernel, f_size, c_size),
        out_shape=jax.ShapeDtypeStruct(tiles.shape[1:], F32),
        in_specs=[VMEM],
        out_specs=VMEM,
        scratch_shapes=[
            pltpu.VMEM((total - 1, *tiles.shape[1:]), F32),
            pltpu.SemaphoreType.DMA((total - 1,)),
            pltpu.SemaphoreType.DMA((total - 1,)),
        ],
        compiler_params=pltpu.CompilerParams(collective_id=collective_id, has_side_effects=True),
        name=f"small_{collective_id}",
    )(tiles)


def normed_of(rows):
    centred = rows - jnp.mean(rows, axis=-1, keepdims=True)
    inv_std = lax.rsqrt(jnp.mean(centred * centred, axis=-1, keepdims=True) + NORM_EPS)
    return centred * inv_std, inv_std


def gelu_both(values):
    tangent = jnp.tanh(GELU_COEF * (values + 0.044715 * values * values * values))
    act = 0.5 * values * (1.0 + tangent)
    slope = 0.5 * (1.0 + tangent) + 0.5 * values * (1.0 - tangent * tangent) * GELU_COEF * (
        1.0 + 3.0 * 0.044715 * values * values
    )
    return act, slope


def rope_tables(count, rot_dim):
    positions = jnp.arange(count, dtype=F32)
    half_dim = rot_dim // 2
    inverse = 10000.0 ** (-(jnp.arange(half_dim, dtype=F32) * 2.0) / rot_dim)
    angles = positions[:, None] * inverse[None, :]
    return (jnp.cos(angles)[:, None, :], jnp.sin(angles)[:, None, :])


def rotate_pairs(values, cosine, sine, rot_dim, sign):
    half_dim = rot_dim // 2
    first_half = values[..., :half_dim]
    second_half = values[..., half_dim:rot_dim]
    return jnp.concatenate(
        [
            first_half * cosine - sign * second_half * sine,
            second_half * cosine + sign * first_half * sine,
            values[..., rot_dim:],
        ],
        axis=-1,
    )


def attention_forward(query, key, value, scale):
    length = query.shape[0]
    block = math.gcd(length, 256)
    contexts, lses = [], []
    for first in range(0, length, block):
        last = first + block
        scores = (
            jnp.einsum("qhd,khd->hqk", query[first:last], key[:last], preferred_element_type=F32)
            * scale
        )
        allowed = jnp.arange(last)[None, :] <= (first + jnp.arange(block))[:, None]
        scores = jnp.where(allowed, scores, MASKED)
        top = jnp.max(scores, axis=-1)
        weights = jnp.where(allowed, jnp.exp(scores - top[..., None]), 0.0)
        total = jnp.sum(weights, axis=-1)
        context = jnp.einsum(
            "hqk,khd->qhd", weights.astype(BF16), value[:last], preferred_element_type=F32
        )
        contexts.append(context / jnp.transpose(total)[..., None])
        lses.append(top + jnp.log(total))
    return jnp.concatenate(contexts, axis=0), jnp.concatenate(lses, axis=1)


def attention_backward(query, key, value, context_grad, delta, lse, scale):
    length, heads, dim = query.shape
    block = math.gcd(length, 256)
    query_grads = []
    key_grad = jnp.zeros((length, heads, dim), F32)
    value_grad = jnp.zeros((length, heads, dim), F32)
    for first in range(0, length, block):
        last = first + block
        q, g = query[first:last], context_grad[first:last]
        scores = jnp.einsum("qhd,khd->hqk", q, key[:last], preferred_element_type=F32) * scale
        allowed = jnp.arange(last)[None, :] <= (first + jnp.arange(block))[:, None]
        probs = jnp.where(allowed, jnp.exp(scores - lse[:, first:last, None]), 0.0)
        value_grad = value_grad.at[:last].add(
            jnp.einsum("hqk,qhd->khd", probs.astype(BF16), g, preferred_element_type=F32)
        )
        prob_grad = jnp.einsum("qhd,khd->hqk", g, value[:last], preferred_element_type=F32)
        score_grad = (probs * (prob_grad - delta[:, first:last, None])).astype(BF16)
        query_grads.append(
            jnp.einsum("hqk,khd->qhd", score_grad, key[:last], preferred_element_type=F32) * scale
        )
        key_grad = key_grad.at[:last].add(
            jnp.einsum("hqk,qhd->khd", score_grad, q, preferred_element_type=F32) * scale
        )
    return jnp.concatenate(query_grads, axis=0), key_grad, value_grad


def body(
    tokens,
    norm_gain,
    norm_bias,
    qkv_weight,
    qkv_bias,
    out_weight,
    out_bias,
    fc1_weight,
    fc1_bias,
    fc2_weight,
    fc2_bias,
    cotangent,
):
    f_size, c_size = lax.axis_size("fsdp"), lax.axis_size("ctx")
    ratio = c_size // f_size
    devices = f_size * c_size
    own_seqs, tok_count, width = tokens.shape
    own_rows = own_seqs * tok_count
    length = tok_count * c_size
    rows = own_seqs * length
    head_dim = HEAD_DIM
    scale = head_dim ** (-0.5)
    row_block = qkv_weight.shape[0]
    cols = qkv_weight.shape[2] // ratio
    hidden_cols = fc1_weight.shape[1] // ratio
    heads = cols // head_dim
    c_index = lax.axis_index("ctx")

    vec = norm_gain.shape[0]
    vec1 = fc1_bias.shape[0]
    def lanes(array):
        array = array.reshape(-1, min(array.shape[-1], 128))
        return jnp.pad(array, ((0, 0), (0, 128 - array.shape[1])))

    small = jnp.concatenate(
        [
            lanes(v)
            for v in (norm_gain, norm_bias, out_bias, fc2_bias, qkv_bias, fc1_bias)
        ]
    )
    small = jnp.pad(small, ((0, -small.shape[0] % 16), (0, 0)))

    qkv_src = (
        jnp.transpose(qkv_weight.reshape(row_block, 3, ratio, cols), (2, 0, 1, 3))
        .reshape(ratio, row_block, 3 * cols)
    )
    fc1_src = jnp.transpose(fc1_weight.reshape(row_block, ratio, hidden_cols), (1, 0, 2))
    out_src = jnp.transpose(out_weight.reshape(ratio, cols, row_block), (0, 2, 1))
    fc2_src = jnp.transpose(fc2_weight.reshape(ratio, hidden_cols, row_block), (0, 2, 1))

    tok_all, cot_all, small_all, qkv_all, fc1_all, fc2_all, out_all = gather_call(
        f_size,
        c_size,
        [tokens.reshape(own_rows, width), cotangent.reshape(own_rows, width)],
        [qkv_src, fc1_src, fc2_src, out_src],
        small,
        0,
    )

    def rows_of(gathered):
        return jnp.swapaxes(gathered.reshape(c_size, own_seqs, tok_count, width), 0, 1).reshape(
            rows, width
        )

    def blocks_of(array):
        return jnp.swapaxes(array.reshape(own_seqs, c_size, tok_count, width), 0, 1).reshape(
            c_size, own_rows, width
        )

    x_rows = rows_of(tok_all)
    grad_rows = rows_of(cot_all)
    qkv_w = qkv_all.reshape(width, 3 * cols)
    fc1_w = fc1_all.reshape(width, hidden_cols)
    out_t = out_all.reshape(width, cols)
    fc2_t = fc2_all.reshape(width, hidden_cols)

    vectors = small_all.reshape(devices, -1, 128)
    gain_full = vectors[:, 0, :vec].reshape(-1).astype(F32)
    shift_full = vectors[:, 1, :vec].reshape(-1).astype(F32)
    out_bias_full = vectors[:, 2, :vec].reshape(-1).astype(F32)
    fc2_bias_full = vectors[:, 3, :vec].reshape(-1).astype(F32)
    qkv_bias_full = jnp.swapaxes(vectors[:, 4:7, :vec], 0, 1).reshape(3, -1)
    lane = min(vec1, 128)
    fc1_bias_full = vectors[:, 7 : 7 + vec1 // lane, :lane].reshape(-1)
    qkv_b = (
        lax.dynamic_slice_in_dim(qkv_bias_full, c_index * cols, cols, 1).reshape(-1).astype(F32)
    )
    fc1_b = lax.dynamic_slice_in_dim(fc1_bias_full, c_index * hidden_cols, hidden_cols, 0).astype(
        F32
    )

    normed, _ = normed_of(x_rows.astype(F32))
    hidden_in = (normed * gain_full + shift_full).astype(BF16)
    mixed = jnp.dot(hidden_in, qkv_w, preferred_element_type=F32) + qkv_b
    cosine, sine = rope_tables(length, ROT_DIM)

    def heads_of(array):
        return array.reshape(own_seqs, length, heads, head_dim)

    query = rotate_pairs(heads_of(mixed[:, :cols]), cosine, sine, ROT_DIM, 1.0).astype(BF16)
    key = rotate_pairs(heads_of(mixed[:, cols : 2 * cols]), cosine, sine, ROT_DIM, 1.0).astype(
        BF16
    )
    value = heads_of(mixed[:, 2 * cols :].astype(BF16))
    forward = [attention_forward(query[s], key[s], value[s], scale) for s in range(own_seqs)]
    context_b = jnp.stack([pair[0] for pair in forward]).astype(BF16)
    context_rows = context_b.reshape(rows, cols)
    pre = jnp.dot(hidden_in, fc1_w, preferred_element_type=F32) + fc1_b
    act, slope = gelu_both(pre)
    act_b = act.astype(BF16)
    contract_last = (((1,), (1,)), ((), ()))
    partial_out = lax.dot_general(
        context_rows, out_t, contract_last, preferred_element_type=F32
    ) + lax.dot_general(act_b, fc2_t, contract_last, preferred_element_type=F32)

    pre_grad = jnp.dot(grad_rows, fc2_t, preferred_element_type=F32) * slope
    pre_grad_b = pre_grad.astype(BF16)
    contract_first = (((0,), (0,)), ((), ()))

    def weight_grad(left, right):
        product = lax.dot_general(left, right, contract_first, preferred_element_type=F32)
        return product.astype(BF16).reshape(ratio, f_size, row_block, right.shape[1])

    fc2_grad = weight_grad(grad_rows, act_b)
    fc1_grad = weight_grad(hidden_in, pre_grad_b)
    out_grad = weight_grad(grad_rows, context_rows)
    fc1_b_grad = jnp.sum(pre_grad, axis=0)
    mlp_back = lax.dot_general(pre_grad_b, fc1_w, contract_last, preferred_element_type=F32)
    context_grad = heads_of(jnp.dot(grad_rows, out_t, preferred_element_type=F32).astype(BF16))
    delta = jnp.swapaxes(
        jnp.sum(context_grad.astype(F32) * context_b.astype(F32), axis=-1), 1, 2
    )
    grads = [
        attention_backward(
            query[s], key[s], value[s], context_grad[s], delta[s], forward[s][1], scale
        )
        for s in range(own_seqs)
    ]
    query_grad, key_grad, value_grad = [jnp.stack(parts) for parts in zip(*grads)]
    mixed_grad = jnp.concatenate(
        [
            rotate_pairs(query_grad, cosine, sine, ROT_DIM, -1.0).reshape(rows, cols),
            rotate_pairs(key_grad, cosine, sine, ROT_DIM, -1.0).reshape(rows, cols),
            value_grad.reshape(rows, cols),
        ],
        axis=1,
    )
    mixed_grad_b = mixed_grad.astype(BF16)
    qkv_grad = weight_grad(hidden_in, mixed_grad_b)
    qkv_b_grad = jnp.sum(mixed_grad, axis=0).reshape(3, cols)
    normed_part = (
        lax.dot_general(mixed_grad_b, qkv_w, contract_last, preferred_element_type=F32) + mlp_back
    )
    (branch, normed_grad), (fc2_shard, fc1_shard, out_shard, qkv_shard) = reduce_all(
        f_size,
        c_size,
        [blocks_of(partial_out.astype(BF16)), blocks_of(normed_part.astype(BF16))],
        [fc2_grad, fc1_grad, out_grad, qkv_grad],
    )

    x_own = tokens.reshape(own_rows, width).astype(F32)
    cot_own = cotangent.reshape(own_rows, width).astype(F32)
    output = (x_own + branch + out_bias_full + fc2_bias_full).astype(BF16)
    normed_own, inv_std_own = normed_of(x_own)
    hat_grad = normed_grad * gain_full
    back_rows = inv_std_own * (
        hat_grad
        - jnp.mean(hat_grad, axis=-1, keepdims=True)
        - normed_own * jnp.mean(hat_grad * normed_own, axis=-1, keepdims=True)
    )
    input_grad = (back_rows + cot_own).astype(BF16)

    def whole(block, full, axis):
        return lax.dynamic_update_slice_in_dim(
            jnp.zeros(full, F32), block, c_index * block.shape[axis], axis
        )

    grad_gain = jnp.sum(normed_grad * normed_own, axis=0).reshape(devices, vec)
    grad_shift = jnp.sum(normed_grad, axis=0).reshape(devices, vec)
    grad_cot = jnp.sum(cot_own, axis=0).reshape(devices, vec)
    q_parts = jnp.swapaxes(whole(qkv_b_grad, (3, width), 1).reshape(3, devices, vec), 0, 1)
    f_parts = whole(fc1_b_grad, (vec1 * devices,), 0).reshape(devices, vec1)
    tiles = jnp.concatenate(
        [grad_gain, grad_shift, grad_cot, q_parts.reshape(devices, 3 * vec), f_parts], axis=1
    )
    used = tiles.shape[1]
    tiles = jnp.pad(tiles, ((0, 0), (0, -used % 1024))).reshape(devices, -1, 128)
    sums = small_call(f_size, c_size, tiles, 4).reshape(-1)

    qkv_out = jnp.transpose(
        qkv_shard.reshape(ratio, row_block, 3, cols), (1, 2, 0, 3)
    ).reshape(row_block, 3, ratio * cols)
    fc1_out = jnp.swapaxes(fc1_shard, 0, 1).reshape(row_block, ratio * hidden_cols)
    out_out = jnp.swapaxes(out_shard, 1, 2).reshape(ratio * cols, row_block)
    fc2_out = jnp.swapaxes(fc2_shard, 1, 2).reshape(ratio * hidden_cols, row_block)
    return (
        output.reshape(own_seqs, tok_count, width),
        input_grad.reshape(own_seqs, tok_count, width),
        sums[:vec],
        sums[vec : 2 * vec],
        qkv_out.astype(F32),
        sums[3 * vec : 6 * vec].reshape(3, vec),
        out_out.astype(F32),
        sums[2 * vec : 3 * vec],
        fc1_out.astype(F32),
        sums[6 * vec : 6 * vec + vec1],
        fc2_out.astype(F32),
        sums[2 * vec : 3 * vec],
    )


def solution(mesh):
    row = P("fsdp", "ctx", None)
    vector = P(("fsdp", "ctx"))
    return jax.shard_map(
        body,
        mesh=mesh,
        in_specs=(
            row,
            vector,
            vector,
            P("ctx", None, "fsdp"),
            P(None, ("fsdp", "ctx")),
            P("fsdp", "ctx"),
            vector,
            P("ctx", "fsdp"),
            vector,
            P("fsdp", "ctx"),
            vector,
            row,
        ),
        out_specs=(
            row,
            row,
            vector,
            vector,
            P("ctx", None, "fsdp"),
            P(None, ("fsdp", "ctx")),
            P("fsdp", "ctx"),
            vector,
            P("ctx", "fsdp"),
            vector,
            P("fsdp", "ctx"),
            vector,
        ),
        check_vma=False,
    )
```

time: 1770 us -> 490 us (0.28)
  waiting for transfers between devices: 1240 us -> 0 us
  Pallas kernels: 0 us -> 341 us
  blocking collectives: 163 us -> 0 us
  starting transfers between devices: 98.5 us -> 0 us
  other arithmetic: 72.2 us -> 24.6 us
  local copies, waits for them, and re-layouts: 68.2 us -> 29.5 us
  matrix products: 108 us -> 86.5 us
    reduce_scatter x6 -> x0, waiting for transfers between devices: 483 us -> none  [the longest x1 148 us: body(): lax.psum_scatter(grad_fc1_w.astype(jnp.bfloat16), 'ctx', scatter_dimensio...]
    all_gather x8 -> x0, waiting for transfers between devices: 439 us -> none  [the longest x1 114 us: body(): lax.all_gather(fc2_weight, 'ctx', axis=1, tiled=True)]
    pallas_call x0 -> x3, Pallas kernels: none -> 341 us  [the longest x1 169 us: gather_call(): pl.pallas_call(functools.partial(gather_kernel, len(acts), len(w_srcs), s...]
    ppermute x16 -> x0, waiting for transfers between devices: 311 us -> none  [the longest x8 286 us: passed_along_2(): return lax.ppermute(value, axis, pairs)]
    unnamed x3 -> x0, blocking collectives: 124 us -> none
    ppermute x16 -> x0, starting transfers between devices: 97.6 us -> none  [the longest x8 58.8 us: passed_along(): lax.ppermute(value, axis, [(source, source + steps) for source in range(f...]
    all_gather x2 -> x0, blocking collectives: 39.4 us -> none  [the longest x1 21.4 us: body(): lax.all_gather(qkv_bias, 'ctx', axis=1, tiled=True)]
    convert_element_type x32 -> x8, other arithmetic: 34.5 us -> 10.1 us  [the longest x2 6.4 us: body(): hidden_in = (normed * gain_full + shift_full).astype(BF16)]
  transfers between devices with their start and end apart: 31 -> 0, of which waited for: 24 -> 0; matrix products, arithmetic and copies ran while one was open for 10% -> 0% of each run, Pallas kernels for 0% -> 0%
where the time goes in v1:
time: 490 us; the launch traced here: 484 us
  Pallas kernels  341 us (70%)
  matrix products  86.5 us (18%)
  local copies, waits for them, and re-layouts  29.5 us (6%)
  other arithmetic  24.6 us (5%)
    pallas_call x1, Pallas kernels, gather_call(): pl.pallas_call(functools.partial(gather_kernel, len(acts), len(w_srcs), s...  169 us
    pallas_call x1, Pallas kernels, reduce_call(): pl.pallas_call(functools.partial(reduce_kernel, len(parts), len(grads), f...  148 us
    pallas_call x1, Pallas kernels, small_call(): pl.pallas_call(functools.partial(small_kernel, f_size, c_size), out_shape...  24.3 us
    dot_general x4, matrix products, weight_grad(): lax.dot_general(left, right, contract_first, preferred_element_type=F32)  20.4 us
    unnamed x78, local copies, waits for them, and re-layouts  11.5 us
    dot_general x1, matrix products, body(): pre_grad = jnp.dot(grad_rows, fc2_t, preferred_element_type=F32) * slope  11.4 us

profile of v1, /device:TPU:0, one launch (start us, length us, event | category | flops | bytes accessed | tf_op | source)
XLA Modules:
  0.0 484.1 jit_solution(11829832095887304355)
XLA Ops:
  0.7 1.5 copy.48
  4.0 1.3 copy.51
  5.3 2.3 copy.52
  9.2 169.2 %gather_0.1 = (bf16[8,128,2048]{2,1,0:T(8,128)(2,1)}, bf16[8,128,2048]{2,1,0:T(8,128)(2,1)}, bf16[4,8,16,128]{3,2,1,0:T(8,128)(2,1)}, bf16[2,4,256,768]{3,2,1,0:...) custom-call(bf16[128,2048]{1,0:T(8,128)(2,1)} %bitcast.273, ...), custom_call_target="tpu_custom_call" | custom-call | tf_op jit(solution)/shard_map/gather_0/pallas_call | solution.py:393
  178.4 3.0 convert_reduce_fusion
  184.0 4.6 add_convert_fusion.2
  188.7 6.5 %fusion.173 = (bf16[1024,768]{0,1:T(8,128)(2,1)S(1)}, f32[1024,768]{0,1:T(8,128)S(1)}) fusion(f32[768]{0:T(1024)S(1)} %reshape.868, bf16[1024,2048]{1,0:T(8,128)(2,1)} %bitcast.280, bf16[2048,768]{1,0:T(8,128)(2,1)} %bitcast.366), kind=kOutput, calls=%fused_computation.250 | convolution fusion | flops 3222798336 | bytes 12061696 | tf_op jit(solution)/shard_map/dot_general | solution.py:985
  203.9 1.5 fusion.11
  213.7 1.8 multiply_convert_fusion
  221.6 1.3 copy-done.1
  222.9 1.8 fusion.3
  224.8 5.2 %convolution_convert_fusion.2 = bf16[2048,768]{1,0:T(8,128)(2,1)} fusion(bf16[1024,2048]{1,0:T(8,128)(2,1)S(1)} %fusion.3, f32[1024,256]{0,1:T(8,128)S(1)} %bitcast.291, f32[1024,256]{0,1:T(8,128)S(1)} %bitcast.287, f32[1024,256]{0,1:T(8,128)S(1)} %bitcast.284), kind=kOutput, calls=%fused_computation.25 | convolution fusion | flops 3227516928 | bytes 10485760 | tf_op jit(solution)/shard_map/dot_general | solution.py:1012
  230.0 2.3 convolution_convert_fusion.3
  232.4 5.7 %fusion.166 = f32[1024,2048]{1,0:T(8,128)} fusion(bf16[2048,768]{1,0:T(8,128)(2,1)S(1)} %bitcast.367, f32[1024,256]{0,1:T(8,128)S(1)} %bitcast.292, f32[1024,256]{0,1:T(8,128)S(1)} %bitcast.288, f32[1024,256]{0,1:T(8,128)S(1)} %bitcast.285), kind=kOutput, calls=%fused_computation.244 | convolution fusion | flops 3225944064 | bytes 14680064 | tf_op jit(solution)/shard_map/dot_general | solution.py:1043
  238.0 6.0 %fusion.175 = f32[1024,1024]{1,0:T(8,128)} fusion(bf16[1024,2048]{1,0:T(8,128)(2,1)S(1)} %bitcast.281, bf16[2048,1024]{1,0:T(8,128)(2,1)S(1)} %bitcast.364), kind=kOutput, calls=%fused_computation.253 | convolution fusion | flops 4294967296 | bytes 12582912 | tf_op jit(solution)/shard_map/dot_general | solution.py:999
  244.1 11.4 %fusion.174 = (f32[1024]{0:T(1024)S(1)}, bf16[1024,1024]{1,0:T(8,128)(2,1)S(1)}) fusion(f32[1024,1024]{1,0:T(8,128)} %fusion.175, f32[1024]{0:T(1024)S(1)} %dynamic-slice_convert_fusion, bf16[1024,2048]{1,0:T(8,128)(2,1)} %bitcast.358, bf16[2048,1024]{1,0:T(8,128)(2,1)} %bitcast.362), kind=kOutput, calls=%fused_computation.251 | convolution fusion | flops 4316986368 | bytes 14688256 | tf_op jit(solution)/shard_map/dot_general | solution.py:1007
  255.6 9.6 %add_convert_fusion = bf16[1024,2048]{1,0:T(8,128)(2,1)} fusion(f32[1024,2048]{1,0:T(8,128)} %fusion.166, bf16[2048,1024]{1,0:T(8,128)(2,1)S(1)} %bitcast.365, bf16[1024,1024]{1,0:T(8,128)(2,1)S(1)} %get-tuple-element.228), kind=kOutput, calls=%fused_computation.5 | convolution fusion | flops 4299161600 | bytes 18874368 | tf_op jit(solution)/shard_map/dot_general | solution.py:1019
  265.2 4.9 %fusion.168 = f32[1024,2048]{1,0:T(8,128)S(1)} fusion(bf16[2048,1024]{1,0:T(8,128)(2,1)S(1)} %bitcast.363, f32[1024,1024]{1,0:T(8,128)S(1)} %copy-done.32, f32[1024]{0:T(1024)S(1)} %dynamic-slice_convert_fusion), kind=kOutput, calls=%fused_computation.245 | convolution fusion | flops 4305453056 | bytes 16781312 | tf_op jit(solution)/shard_map/dot_general | solution.py:1005
  270.1 3.4 add_convert_fusion.1
  274.1 6.2 %convolution_convert_fusion = bf16[2048,1024]{1,0:T(8,128)(2,1)} fusion(bf16[1024,2048]{1,0:T(8,128)(2,1)S(1)} %copy-done.5, bf16[1024,1024]{1,0:T(8,128)(2,1)S(1)} %copy-done.34), kind=kOutput, calls=%fused_computation.23 | convolution fusion | flops 4297064448 | bytes 10485760 | tf_op jit(solution)/shard_map/dot_general | solution.py:1012
  280.3 6.7 %convolution_convert_fusion.1 = bf16[2048,1024]{1,0:T(8,128)(2,1)} fusion(bf16[1024,2048]{1,0:T(8,128)(2,1)S(1)} %bitcast.361, f32[1024,1024]{1,0:T(8,128)S(1)} %copy-done.32, f32[1024]{0:T(1024)S(1)} %dynamic-slice_convert_fusion), kind=kOutput, calls=%fused_computation.24 | convolution fusion | flops 4307550208 | bytes 12587008 | tf_op jit(solution)/shard_map/dot_general | solution.py:1012
  287.0 147.9 %reduce_2.1 = (f32[128,2048]{1,0:T(8,128)}, f32[128,2048]{1,0:T(8,128)}, bf16[2,256,1024]{2,1,0:T(8,128)(2,1)}, bf16[2,256,1024]{2,1,0:T(8,128)(2,1)}, bf16[2,25...) custom-call(bf16[8,128,2048]{2,1,0:T(8,128)(2,1)} %bitcast.272, bf16[8,128,2048]{2,1,0:T(8,128)(2,1)} %bitcast.277, ...), custom_call_target="tpu_custom_call" | custom-call | tf_op jit(solution)/shard_map/reduce_2/pallas_call | solution.py:729
  434.9 1.5 convert_bitcast_fusion.1
  436.4 1.8 copy.65
  438.2 2.9 copy.68
  441.5 1.6 copy.67
  443.1 1.5 convert_bitcast_fusion
  444.6 1.8 copy.66
  446.4 2.2 fusion.16
  450.8 1.7 convert_reduce_fusion.2
  453.8 24.3 %small_4.1 = f32[8,128]{1,0:T(8,128)} custom-call(f32[32,8,128]{2,1,0:T(8,128)} %bitcast.329), custom_call_target="tpu_custom_call" | custom-call | tf_op jit(solution)/shard_map/small_4/pallas_call | solution.py:790
  479.4 1.4 fusion.172
  (187 shorter events, 37.4 us)
Async XLA Ops:
  0.6 2.8 copy-start.12
  2.2 5.3 %copy-start.16 = (bf16[512,256]{1,0:T(8,128)(2,1)S(1)}, bf16[512,256]{1,0:T(8,128)(2,1)}, u32[]{:S(2)}) copy-start(bf16[512,256]{1,0:T(8,128)(2,1)} %param.37) | copy-start | bytes 786436
  2.2 6.2 %copy-start.19 = (bf16[3,64]{1,0:T(4,128)(2,1)S(1)}, bf16[3,64]{1,0:T(4,128)(2,1)}, u32[]{:S(2)}) copy-start(bf16[3,64]{1,0:T(4,128)(2,1)} %param.36) | copy-start | bytes 1156
  2.2 6.2 %copy-start.28 = (bf16[64]{0:T(256)(128)(2,1)S(1)}, bf16[64]{0:T(256)(128)(2,1)}, u32[]{:S(2)}) copy-start(bf16[64]{0:T(256)(128)(2,1)} %param.33) | copy-start | bytes 388
  2.2 6.2 %copy-start.29 = (bf16[64]{0:T(256)(128)(2,1)S(1)}, bf16[64]{0:T(256)(128)(2,1)}, u32[]{:S(2)}) copy-start(bf16[64]{0:T(256)(128)(2,1)} %param.34) | copy-start | bytes 388
  2.3 6.2 %copy-start.30 = (bf16[64]{0:T(256)(128)(2,1)S(1)}, bf16[64]{0:T(256)(128)(2,1)}, u32[]{:S(2)}) copy-start(bf16[64]{0:T(256)(128)(2,1)} %param.38) | copy-start | bytes 388
  2.3 6.2 %copy-start.31 = (bf16[64]{0:T(256)(128)(2,1)S(1)}, bf16[64]{0:T(256)(128)(2,1)}, u32[]{:S(2)}) copy-start(bf16[64]{0:T(256)(128)(2,1)} %param.42) | copy-start | bytes 388
  2.3 6.2 %copy-start.21 = (bf16[256]{0:T(256)(128)(2,1)S(1)}, bf16[256]{0:T(256)(128)(2,1)}, u32[]{:S(2)}) copy-start(bf16[256]{0:T(256)(128)(2,1)} %param.40) | copy-start | bytes 1540
  178.4 3.5 copy-start
  178.4 4.7 copy-start.17
  205.4 2.5 copy-start.22
  218.3 14.1 %copy-start.6 = (f32[1,1024,4,64]{1,3,2,0:T(8,128)}, f32[1,1024,4,64]{1,3,2,0:T(8,128)S(1)}, u32[]{:S(2)}) copy-start(f32[1,1024,4,64]{1,3,2,0:T(8,128)S(1)} %pad_maximum_fusion.1) | copy-start | bytes 3145732
  218.4 14.0 %copy-start.7 = (f32[1,1024,4,64]{1,3,2,0:T(8,128)}, f32[1,1024,4,64]{1,3,2,0:T(8,128)S(1)}, u32[]{:S(2)}) copy-start(f32[1,1024,4,64]{1,3,2,0:T(8,128)S(1)} %pad_maximum_fusion.2) | copy-start | bytes 3145732
  221.6 10.8 %copy-start.8 = (f32[1024,4,64]{0,2,1:T(8,128)}, f32[1024,4,64]{0,2,1:T(8,128)S(1)}, u32[]{:S(2)}) copy-start(f32[1024,4,64]{0,2,1:T(8,128)S(1)} %fusion.43) | copy-start | bytes 3145732
  224.8 5.2 %copy-start.4 = (bf16[1024,2048]{1,0:T(8,128)(2,1)}, bf16[1024,2048]{1,0:T(8,128)(2,1)S(1)}, u32[]{:S(2)}) copy-start(bf16[1024,2048]{1,0:T(8,128)(2,1)S(1)} %fusion.3) | copy-start | bytes 12582916
  232.4 5.7 %copy-start.3 = (bf16[8,128,2048]{2,1,0:T(8,128)(2,1)S(1)}, bf16[8,128,2048]{2,1,0:T(8,128)(2,1)}, u32[]{:S(2)}) copy-start(bf16[8,128,2048]{2,1,0:T(8,128)(2,1)} %add_convert_fusion.2) | copy-start | bytes 12582916
  232.4 5.7 %copy-start.25 = (bf16[2,4,256,1024]{3,2,1,0:T(8,128)(2,1)S(1)}, bf16[2,4,256,1024]{3,2,1,0:T(8,128)(2,1)}, u32[]{:S(2)}) copy-start(bf16[2,4,256,1024]{3,2,1,0:T(8,128)(2,1)} %get-tuple-element.141) | copy-start | bytes 12582916
  244.1 11.5 %copy-start.26 = (bf16[2,4,256,1024]{3,2,1,0:T(8,128)(2,1)S(1)}, bf16[2,4,256,1024]{3,2,1,0:T(8,128)(2,1)}, u32[]{:S(2)}) copy-start(bf16[2,4,256,1024]{3,2,1,0:T(8,128)(2,1)} %get-tuple-element.141) | copy-start | bytes 12582916
  255.6 9.6 %copy-start.33 = (bf16[1024,1024]{1,0:T(8,128)(2,1)}, bf16[1024,1024]{1,0:T(8,128)(2,1)S(1)}, u32[]{:S(2)}) copy-start(bf16[1024,1024]{1,0:T(8,128)(2,1)S(1)} %get-tuple-element.228) | copy-start | bytes 6291460
  255.6 9.6 %copy-start.24 = (bf16[2,4,256,1024]{3,2,1,0:T(8,128)(2,1)S(1)}, bf16[2,4,256,1024]{3,2,1,0:T(8,128)(2,1)}, u32[]{:S(2)}) copy-start(bf16[2,4,256,1024]{3,2,1,0:T(8,128)(2,1)} %get-tuple-element.142) | copy-start | bytes 12582916
  255.6 9.6 %copy-start.32 = (f32[1024,1024]{1,0:T(8,128)S(1)}, f32[1024,1024]{1,0:T(8,128)}, u32[]{:S(2)}) copy-start(f32[1024,1024]{1,0:T(8,128)} %fusion.175) | copy-start | bytes 12582916
  270.1 3.4 copy-start.5
  270.1 4.0 copy-start.34
  274.1 6.2 %copy-start.23 = (bf16[8,128,2048]{2,1,0:T(8,128)(2,1)S(1)}, bf16[8,128,2048]{2,1,0:T(8,128)(2,1)}, u32[]{:S(2)}) copy-start(bf16[8,128,2048]{2,1,0:T(8,128)(2,1)} %get-tuple-element.143) | copy-start | bytes 12582916
  436.3 4.7 copy-start.14
  444.6 4.4 copy-start.2
  444.6 6.1 %copy-start.18 = (f32[32,64]{1,0:T(8,128)S(1)}, f32[32,64]{1,0:T(8,128)}, u32[]{:S(2)}) copy-start(f32[32,64]{1,0:T(8,128)} %get-tuple-element.179) | copy-start | bytes 24580
  444.6 6.2 %copy-start.10 = (bf16[1,128,2048]{2,1,0:T(8,128)(2,1)S(1)}, bf16[1,128,2048]{2,1,0:T(8,128)(2,1)}, u32[]{:S(2)}) copy-start(bf16[1,128,2048]{2,1,0:T(8,128)(2,1)} %param.43) | copy-start | bytes 1572868
  446.4 3.0 copy-start.9
  446.4 4.3 copy-start.13
  448.7 33.4 %copy-start.15 = (bf16[2,256,256]{2,1,0:T(8,128)(2,1)S(1)}, bf16[2,256,256]{2,1,0:T(8,128)(2,1)}, u32[]{:S(2)}) copy-start(bf16[2,256,256]{2,1,0:T(8,128)(2,1)} %get-tuple-element.147) | copy-start | bytes 786436
  480.8 2.8 copy-start.20
  (3 other events, 6.1 us)

commit v2 on v1

--- a/solution.py
+++ b/solution.py
@@ -738,17 +738,6 @@
     return outs[: len(parts)], outs[len(parts) :]
 
 
-def reduce_all(f_size, c_size, parts, grads):
-    size = sum(2.25 * part.size * part.dtype.itemsize for part in parts)
-    size += sum(2.5 * grad.size * grad.dtype.itemsize for grad in grads)
-    if size <= 56 * 2**20:
-        return reduce_call(f_size, c_size, parts, grads, 2)
-    half = len(grads) // 2
-    (first,), early = reduce_call(f_size, c_size, parts[:1], grads[:half], 2)
-    (second,), late = reduce_call(f_size, c_size, parts[1:], grads[half:], 3)
-    return (first, second), (*early, *late)
-
-
 def small_kernel(f_size, c_size, tiles, out, held, send_sem, recv_sem):
     fs, cx = Axis("fsdp", f_size), Axis("ctx", c_size)
     total = f_size * c_size
@@ -939,10 +928,11 @@
     out_src = jnp.transpose(out_weight.reshape(ratio, cols, row_block), (0, 2, 1))
     fc2_src = jnp.transpose(fc2_weight.reshape(ratio, hidden_cols, row_block), (0, 2, 1))
 
-    tok_all, cot_all, small_all, qkv_all, fc1_all, fc2_all, out_all = gather_call(
+    grad_rows = lax.all_gather(cotangent, "ctx", axis=1, tiled=True).reshape(rows, width)
+    tok_all, small_all, qkv_all, fc1_all, fc2_all, out_all = gather_call(
         f_size,
         c_size,
-        [tokens.reshape(own_rows, width), cotangent.reshape(own_rows, width)],
+        [tokens.reshape(own_rows, width)],
         [qkv_src, fc1_src, fc2_src, out_src],
         small,
         0,
@@ -959,7 +949,6 @@
         )
 
     x_rows = rows_of(tok_all)
-    grad_rows = rows_of(cot_all)
     qkv_w = qkv_all.reshape(width, 3 * cols)
     fc1_w = fc1_all.reshape(width, hidden_cols)
     out_t = out_all.reshape(width, cols)
@@ -1042,11 +1031,22 @@
     normed_part = (
         lax.dot_general(mixed_grad_b, qkv_w, contract_last, preferred_element_type=F32) + mlp_back
     )
-    (branch, normed_grad), (fc2_shard, fc1_shard, out_shard, qkv_shard) = reduce_all(
+    branch = (
+        lax.psum_scatter(
+            partial_out.astype(BF16).reshape(own_seqs, length, width),
+            "ctx",
+            scatter_dimension=1,
+            tiled=True,
+        )
+        .reshape(own_rows, width)
+        .astype(F32)
+    )
+    (normed_grad,), (fc2_shard, fc1_shard, out_shard, qkv_shard) = reduce_call(
         f_size,
         c_size,
-        [blocks_of(partial_out.astype(BF16)), blocks_of(normed_part.astype(BF16))],
+        [blocks_of(normed_part.astype(BF16))],
         [fc2_grad, fc1_grad, out_grad, qkv_grad],
+        2,
     )
 
     x_own = tokens.reshape(own_rows, width).astype(F32)

time: 490 us -> 526 us (1.073)
  local copies, waits for them, and re-layouts: 29.5 us -> 50.8 us
  other arithmetic: 24.6 us -> 43.3 us
  between operations: 2.06 us -> 16.3 us
  Pallas kernels: 341 us -> 329 us
  matrix products: 86.5 us -> 80.5 us
    pallas_call x1, Pallas kernels: 148 us -> 120 us  [reduce_call(): pl.pallas_call(functools.partial(reduce_kernel, len(parts), len(grads), f...]
    pallas_call x1, Pallas kernels: 169 us -> 186 us  [gather_call(): pl.pallas_call(functools.partial(gather_kernel, len(acts), len(w_srcs), s...]
    convert_element_type x0 -> x2, local copies, waits for them, and re-layouts: none -> 8.07 us  [weight_grad(): product.astype(BF16).reshape(ratio, f_size, row_block, right.shape[1])]
    unnamed x78 -> x226, local copies, waits for them, and re-layouts: 11.5 us -> 15.1 us
  transfers between devices with their start and end apart: 0 -> 2, of which waited for: 0 -> 0; matrix products, arithmetic and copies ran while one was open for 0% -> 32% of each run, Pallas kernels for 0% -> 63%
where the time goes in v2:
time: 526 us; the launch traced here: 521 us
  Pallas kernels  329 us (63%)
  matrix products  80.5 us (15%)
  local copies, waits for them, and re-layouts  50.8 us (10%)
  other arithmetic  43.3 us (8%)
  between operations  16.3 us (3%)
    pallas_call x1, Pallas kernels, gather_call(): pl.pallas_call(functools.partial(gather_kernel, len(acts), len(w_srcs), s...  186 us
    pallas_call x1, Pallas kernels, reduce_call(): pl.pallas_call(functools.partial(reduce_kernel, len(parts), len(grads), f...  120 us
    dot_general x4, matrix products, weight_grad(): lax.dot_general(left, right, contract_first, preferred_element_type=F32)  23.4 us
    pallas_call x1, Pallas kernels, small_call(): pl.pallas_call(functools.partial(small_kernel, f_size, c_size), out_shape...  22.9 us
    unnamed x226, local copies, waits for them, and re-layouts  15.1 us
  transfers between devices with their start and end apart: 2, of which 0 were waited for; matrix products, arithmetic and copies ran while one was open for 32% of the time, Pallas kernels for 63%

profile of v2, /device:TPU:0, one launch (start us, length us, event | category | flops | bytes accessed | tf_op | source)
XLA Modules:
  0.0 520.8 jit_solution(4121383407912585422)
XLA Ops:
  12.5 2.3 copy.56
  16.5 185.7 %gather_0.1 = (bf16[8,128,2048]{2,1,0:T(8,128)(2,1)}, bf16[4,8,16,128]{3,2,1,0:T(8,128)(2,1)}, bf16[2,4,256,768]{3,2,1,0:T(8,128)(2,1)}, bf16[2,4,256,1024]{3,2,...) custom-call(bf16[128,2048]{1,0:T(8,128)(2,1)} %bitcast.297, ...), custom_call_target="tpu_custom_call" | custom-call | tf_op jit(solution)/shard_map/gather_0/pallas_call | solution.py:393
  202.1 1.9 fusion.157
  206.7 2.8 convert_reduce_fusion
  212.2 3.7 add_convert_fusion.2
  216.0 3.7 fusion.192
  226.3 1.5 slice.460
  239.2 1.9 fusion.22
  244.6 4.5 fusion.194
  249.1 4.9 fusion.187
  254.1 3.3 fusion.20
  263.7 4.8 fusion.3
  268.5 3.9 fusion.75
  278.1 1.8 multiply_convert_fusion
  287.9 1.5 copy.66
  289.4 10.8 %convert_bitcast_fusion = bf16[2048,1024]{0,1:T(8,128)(2,1)} fusion(bf16[1,1024,2048]{2,1,0:T(8,128)(2,1)} %all-gather.2.cloned.1.call-done, f32[1024,1024]{1,0:T(8,128)} %copy-done.108, f32[1024]{0:T(1024)S(1)} %copy-done.90), kind=kOutput, calls=%fused_computation.26 | convolution fusion | flops 4307550208 | bytes 12587008 | tf_op jit(solution)/shard_map/dot_general | solution.py:1001
  300.3 6.6 %copy.65 = bf16[2048,1024]{1,0:T(8,128)(2,1)} copy(bf16[2048,1024]{0,1:T(8,128)(2,1)} %convert_bitcast_fusion) | data formatting | bytes 8388608 | tf_op jit(solution)/shard_map/convert_element_type | solution.py:1002
  307.0 1.7 pad_maximum_fusion.2
  311.0 3.5 fusion.185
  314.6 5.0 convolution_convert_fusion.1
  319.5 8.8 %fusion.193 = (f32[1024]{0:T(1024)S(1)}, bf16[1024,1024]{1,0:T(8,128)(2,1)S(1)}) fusion(f32[1024,1024]{1,0:T(8,128)} %copy-done.108, f32[1024]{0:T(1024)S(1)} %copy-done.91, bf16[2048,1024]{1,0:T(8,128)(2,1)S(1)} %bitcast.385, bf16[1,1024,2048]{2,1,0:T(8,128)(2,1)S(1)} %copy-done.97), kind=kOutput, calls=%fused_computation.258 | convolution fusion | flops 4316986368 | bytes 14688256 | tf_op jit(solution)/shard_map/dot_general | solution.py:996
  328.4 6.3 %convolution_convert_fusion = bf16[2048,1024]{1,0:T(8,128)(2,1)} fusion(bf16[1024,2048]{1,0:T(8,128)(2,1)S(1)} %copy-done.10, bf16[1024,1024]{1,0:T(8,128)(2,1)S(1)} %get-tuple-element.221), kind=kOutput, calls=%fused_computation.32 | convolution fusion | flops 4297064448 | bytes 10485760 | tf_op jit(solution)/shard_map/dot_general | solution.py:1001
  334.7 6.3 %add_convert_fusion = bf16[1024,2048]{1,0:T(8,128)(2,1)} fusion(f32[1024,2048]{1,0:T(8,128)S(1)} %fusion.185, bf16[2048,1024]{1,0:T(8,128)(2,1)S(1)} %bitcast.383, bf16[1024,1024]{1,0:T(8,128)(2,1)S(1)} %get-tuple-element.221), kind=kOutput, calls=%fused_computation.5 | convolution fusion | flops 4299161600 | bytes 18874368 | tf_op jit(solution)/shard_map/dot_general | solution.py:1008
  340.9 120.5 %reduce_2.1 = (f32[128,2048]{1,0:T(8,128)}, bf16[2,256,1024]{2,1,0:T(8,128)(2,1)}, bf16[2,256,1024]{2,1,0:T(8,128)(2,1)}, bf16[2,256,256]{2,1,0:T(8,128)(2,1)}, bf16[2,256,768]{2,1,0:T(8,128)(2,1)}) custom-call(bf16[8,128,2048]{2,1,0:T(8,128)(2,1)} %bitcast.321, bf16[2,4,256,1024]{3,2,1,0:T(8,128)(2,1)} %bitcast.298, bf16[2,4,256,1024]{3,2,1,0:T(8,128)(2,1)} %bitcast.320, ...), custom_call_target="tpu_custom_call" | custom-call | tf_op jit(solution)/shard_map/reduce_2/pallas_call | solution.py:729
  461.4 1.5 convert_bitcast_fusion.2
  462.9 2.1 copy.71
  465.0 2.9 copy.74
  470.6 3.0 copy.73
  475.1 1.8 copy.72
  476.9 2.2 fusion.33
  481.7 22.9 %small_4.1 = f32[8,128]{1,0:T(8,128)} custom-call(f32[32,8,128]{2,1,0:T(8,128)} %bitcast.353), custom_call_target="tpu_custom_call" | custom-call | tf_op jit(solution)/shard_map/small_4/pallas_call | solution.py:779
  510.9 2.0 add_convert_fusion.3
  (346 shorter events, 68.5 us)
Async XLA Ops:
  7.2 261.3 %all-gather.2.cloned.1.call-start = ((), (), s32[]{:S(2)}) async-start(), calls=%async_computation.2 | async-start | bytes 4718592 | tf_op jit(solution)/shard_map/all_gather | solution.py:931
  7.9 503.0 %reduce-scatter.2.cloned.1.call-start = ((), (), s32[]{:S(2)}) async-start(), calls=%async_computation.1 | async-start | bytes 4718592 | tf_op jit(solution)/shard_map/reduce_scatter | solution.py:1035
  9.5 6.2 %copy-start.93 = (bf16[3,64]{1,0:T(4,128)(2,1)S(1)}, bf16[3,64]{1,0:T(4,128)(2,1)}, u32[]{:S(2)}) copy-start(bf16[3,64]{1,0:T(4,128)(2,1)} %param.36) | copy-start | bytes 1156
  9.5 6.2 %copy-start.104 = (bf16[64]{0:T(256)(128)(2,1)S(1)}, bf16[64]{0:T(256)(128)(2,1)}, u32[]{:S(2)}) copy-start(bf16[64]{0:T(256)(128)(2,1)} %param.33) | copy-start | bytes 388
  9.5 6.2 %copy-start.105 = (bf16[64]{0:T(256)(128)(2,1)S(1)}, bf16[64]{0:T(256)(128)(2,1)}, u32[]{:S(2)}) copy-start(bf16[64]{0:T(256)(128)(2,1)} %param.34) | copy-start | bytes 388
  9.5 6.2 %copy-start.106 = (bf16[64]{0:T(256)(128)(2,1)S(1)}, bf16[64]{0:T(256)(128)(2,1)}, u32[]{:S(2)}) copy-start(bf16[64]{0:T(256)(128)(2,1)} %param.38) | copy-start | bytes 388
  9.5 6.2 %copy-start.107 = (bf16[64]{0:T(256)(128)(2,1)S(1)}, bf16[64]{0:T(256)(128)(2,1)}, u32[]{:S(2)}) copy-start(bf16[64]{0:T(256)(128)(2,1)} %param.42) | copy-start | bytes 388
  9.5 6.2 %copy-start.95 = (bf16[256]{0:T(256)(128)(2,1)S(1)}, bf16[256]{0:T(256)(128)(2,1)}, u32[]{:S(2)}) copy-start(bf16[256]{0:T(256)(128)(2,1)} %param.40) | copy-start | bytes 1540
  202.1 8.0 %copy-start = (bf16[8,128,2048]{2,1,0:T(8,128)(2,1)S(1)}, bf16[8,128,2048]{2,1,0:T(8,128)(2,1)}, u32[]{:S(2)}) copy-start(bf16[8,128,2048]{2,1,0:T(8,128)(2,1)} %get-tuple-element.135) | copy-start | bytes 12582916
  221.0 8.3 %copy-start.24 = (bf16[1,1024,4,16]{1,3,2,0:T(8,128)(2,1)}, bf16[1,1024,4,16]{1,3,2,0:T(8,128)(2,1)S(1)}, u32[]{:S(2)}) copy-start(bf16[1,1024,4,16]{1,3,2,0:T(8,128)(2,1)S(1)} %get-tuple-element.195) | copy-start | bytes 393220
  221.4 7.9 %copy-start.27 = (bf16[256,4,64]{0,2,1:T(8,128)(2,1)}, bf16[256,4,64]{0,2,1:T(8,128)(2,1)S(1)}, u32[]{:S(2)}) copy-start(bf16[256,4,64]{0,2,1:T(8,128)(2,1)S(1)} %maximum_bitcast_fusion.1) | copy-start | bytes 393220
  221.5 13.4 %copy-start.20 = (bf16[1,1024,4,64]{1,3,2,0:T(8,128)(2,1)}, bf16[1,1024,4,64]{1,3,2,0:T(8,128)(2,1)S(1)}, u32[]{:S(2)}) copy-start(bf16[1,1024,4,64]{1,3,2,0:T(8,128)(2,1)S(1)} %get-tuple-element.223) | copy-start | bytes 1572868
  221.5 14.3 %copy-start.18 = (bf16[1,1024,4,64]{1,3,2,0:T(8,128)(2,1)}, bf16[1,1024,4,64]{1,3,2,0:T(8,128)(2,1)S(1)}, u32[]{:S(2)}) copy-start(bf16[1,1024,4,64]{1,3,2,0:T(8,128)(2,1)S(1)} %get-tuple-element.222) | copy-start | bytes 1572868
  228.6 20.6 %copy-start.89 = (f32[1024]{0:T(1024)}, f32[1024]{0:T(1024)S(1)}, u32[]{:S(2)}) copy-start(f32[1024]{0:T(1024)S(1)} %dynamic-slice_convert_fusion) | copy-start | bytes 12292
  230.2 7.8 %copy-start.22 = (pred[256,768]{1,0:T(8,128)(4,1)}, pred[256,768]{1,0:T(8,128)(4,1)S(1)}, u32[]{:S(2)}) copy-start(pred[256,768]{1,0:T(8,128)(4,1)S(1)} %iota_compare_fusion.1) | copy-start | bytes 589828
  232.7 21.4 %copy-start.39 = (bf16[256,4,64]{0,2,1:T(8,128)(2,1)}, bf16[256,4,64]{0,2,1:T(8,128)(2,1)S(1)}, u32[]{:S(2)}) copy-start(bf16[256,4,64]{0,2,1:T(8,128)(2,1)S(1)} %fusion.104) | copy-start | bytes 393220
  234.9 19.2 %copy-start.41 = (bf16[256,4,64]{0,2,1:T(8,128)(2,1)}, bf16[256,4,64]{0,2,1:T(8,128)(2,1)S(1)}, u32[]{:S(2)}) copy-start(bf16[256,4,64]{0,2,1:T(8,128)(2,1)S(1)} %fusion.105) | copy-start | bytes 393220
  239.1 15.0 %copy-start.43 = (bf16[256,4,64]{0,2,1:T(8,128)(2,1)}, bf16[256,4,64]{0,2,1:T(8,128)(2,1)S(1)}, u32[]{:S(2)}) copy-start(bf16[256,4,64]{0,2,1:T(8,128)(2,1)S(1)} %fusion.109) | copy-start | bytes 393220
  242.4 11.7 %copy-start.45 = (bf16[256,4,64]{0,2,1:T(8,128)(2,1)}, bf16[256,4,64]{0,2,1:T(8,128)(2,1)S(1)}, u32[]{:S(2)}) copy-start(bf16[256,4,64]{0,2,1:T(8,128)(2,1)S(1)} %fusion.115) | copy-start | bytes 393220
  257.6 6.1 %copy-start.68 = (f32[1024]{0:T(1024)S(1)}, f32[1024]{0:T(1024)}, u32[]{:S(2)}) copy-start(f32[1024]{0:T(1024)} %get-tuple-element.203) | copy-start | bytes 12292
  260.8 7.6 %copy-start.87 = (f32[128]{0:T(128)}, f32[128]{0:T(128)S(1)}, u32[]{:S(2)}) copy-start(f32[128]{0:T(128)S(1)} %broadcast_multiply_fusion.4) | copy-start | bytes 1540
  300.3 6.6 %slice-start = ((f32[1,1024,4,64]{1,3,2,0:T(8,128)}), f32[1,1024,4,32]{1,3,2,0:T(8,128)S(1)}, s32[]{:S(2)}) async-start(f32[1,1024,4,64]{1,3,2,0:T(8,128)} %copy-done.13), calls=%async_computation.3 | async-start | bytes 1048576 | tf_op jit(solution)/shard_map/slice | solution.py:825
  300.3 6.6 %copy-start.33 = (f32[1,1024,4,16]{1,3,2,0:T(8,128)S(1)}, f32[1,1024,4,16]{1,3,2,0:T(8,128)}, u32[]{:S(2)}) copy-start(f32[1,1024,4,16]{1,3,2,0:T(8,128)} %get-tuple-element.180) | copy-start | bytes 786436
  300.3 6.6 %copy-start.34 = (f32[1,1024,4,16]{1,3,2,0:T(8,128)S(1)}, f32[1,1024,4,16]{1,3,2,0:T(8,128)}, u32[]{:S(2)}) copy-start(f32[1,1024,4,16]{1,3,2,0:T(8,128)} %get-tuple-element.181) | copy-start | bytes 786436
  300.3 8.4 %copy-start.50 = (bf16[256,256]{0,1:T(8,128)(2,1)S(1)}, bf16[256,256]{0,1:T(8,128)(2,1)}, u32[]{:S(2)}) copy-start(bf16[256,256]{0,1:T(8,128)(2,1)} %copy-done.49) | copy-start | bytes 393220
  307.0 7.5 %copy-start.15 = (f32[1,1024,4,64]{1,3,2,0:T(8,128)}, f32[1,1024,4,64]{1,3,2,0:T(8,128)S(1)}, u32[]{:S(2)}) copy-start(f32[1,1024,4,64]{1,3,2,0:T(8,128)S(1)} %pad_maximum_fusion.1) | copy-start | bytes 3145732
  328.4 6.3 %copy-start.99 = (bf16[2,4,256,1024]{3,2,1,0:T(8,128)(2,1)S(1)}, bf16[2,4,256,1024]{3,2,1,0:T(8,128)(2,1)}, u32[]{:S(2)}) copy-start(bf16[2,4,256,1024]{3,2,1,0:T(8,128)(2,1)} %get-tuple-element.139) | copy-start | bytes 12582916
  475.1 32.2 %copy-start.53 = (bf16[2,256,256]{2,1,0:T(8,128)(2,1)S(1)}, bf16[2,256,256]{2,1,0:T(8,128)(2,1)}, u32[]{:S(2)}) copy-start(bf16[2,256,256]{2,1,0:T(8,128)(2,1)} %get-tuple-element.143) | copy-start | bytes 786436
  476.9 32.7 %copy-start.92 = (f32[128]{0:T(128)S(1)}, f32[128]{0:T(128)}, u32[]{:S(2)}) copy-start(f32[128]{0:T(128)} %add_rsqrt_fusion.1) | copy-start | bytes 1540
  479.1 31.8 %copy-start.66 = (f32[2048]{0:T(1024)S(1)}, f32[2048]{0:T(1024)}, u32[]{:S(2)}) copy-start(f32[2048]{0:T(1024)} %reshape.884) | copy-start | bytes 24580
  479.1 31.8 %copy-start.67 = (f32[2048]{0:T(1024)S(1)}, f32[2048]{0:T(1024)}, u32[]{:S(2)}) copy-start(f32[2048]{0:T(1024)} %reshape.885) | copy-start | bytes 24580
  507.3 6.2 %copy-start.94 = (f32[64]{0:T(128)}, f32[64]{0:T(128)S(1)}, u32[]{:S(2)}) copy-start(f32[64]{0:T(128)S(1)} %get-tuple-element.249) | copy-start | bytes 772
  (80 other events, 247.4 us)
Sparse Core Ops, SparseCore 0:
  10.1 125.6 all-gather.1
  257.7 89.4 reduce-scatter.1

commit v3 on v1

--- a/solution.py
+++ b/solution.py
@@ -3,6 +3,7 @@
 
 import jax
 import jax.numpy as jnp
+import numpy as np
 from jax import lax
 from jax.experimental import pallas as pl
 from jax.experimental.pallas import tpu as pltpu
@@ -231,23 +232,30 @@
     return lax.rem(device + fs.size - shift_of(column, fs.size), fs.size)
 
 
-def gather_kernel(n_act, n_w, small, f_size, c_size, *refs):
+def gather_kernel(n_act, n_w, fused, f_size, c_size, *refs):
     fs, cx = Axis("fsdp", f_size), Axis("ctx", c_size)
     ratio = c_size // f_size
-    n_ctx = n_act + (1 if small else 0)
-    n_in = n_ctx + n_w
-    ins, outs, rest = refs[:n_in], refs[n_in : 2 * n_in], list(refs[2 * n_in :])
-    acts, w_srcs = ins[:n_ctx], ins[n_ctx:]
-    act_outs, w_outs = outs[:n_ctx], outs[n_ctx:]
+    total = f_size * c_size
+    me = fs.me * c_size + cx.me
+    n_extra = 2 if fused else 0
+    n_in = n_act + 1 + n_w + n_extra
+    ins, refs = refs[:n_in], refs[n_in:]
+    acts, small_own, w_srcs = ins[:n_act], ins[n_act], ins[n_act + 1 : n_act + 1 + n_w]
+    n_out = n_act + 1 + n_w + (5 if fused else 0)
+    outs, rest = refs[:n_out], list(refs[n_out:])
+    act_outs, small_out, w_outs = outs[:n_act], outs[n_act], outs[n_act + 1 : n_act + 1 + n_w]
+    if fused:
+        tables = ins[n_act + 1 + n_w :]
+        query, key, value, context, lse = outs[n_act + 1 + n_w :]
+    small_send, small_recv = rest[:2]
+    rest = rest[2:]
     own_sem = rest.pop(0)
     lines = []
-    for index in range(n_ctx):
+    for index in range(n_act):
         out = act_outs[index]
-        if index < n_act:
-            slot = lambda c, out=out: out.at[c]
-        else:
-            slot = lambda c, out=out: out.at[fs.me, c]
-        lines.append(Line(cx, slot, acts[index], *rest[:6]))
+        slot = lambda c, out=out: out.at[c]
+        source = slot(cx.me) if fused and index == 0 else acts[index]
+        lines.append(Line(cx, slot, source, *rest[:6]))
         rest = rest[6:]
     mids, rest = rest[:n_w], rest[n_w:]
     mid_send, mid_recv, w_send, w_recv = rest[:4]
@@ -259,11 +267,6 @@
         slot = lambda f, out=out: out.at[:, low_slot(fs, column, f)]
         spreads.append(Spread(fs, slot, slot(fs.me), *rest[:4]))
         rest = rest[4:]
-    if small:
-        out = act_outs[n_act]
-        slot = lambda f, out=out: out.at[f]
-        small_spread = Spread(fs, slot, slot(fs.me), *rest[:4])
-
     pass_to = lax.rem(cx.me + shift_of(fs.me, f_size), f_size)
     pass_from = unshift(lax.rem(fs.me + f_size - lax.rem(cx.me, f_size), f_size), f_size)
     stays = pass_to == fs.me
@@ -310,53 +313,160 @@
         for step in range(1, fs.high):
             spreads[index].forward(step)
 
+    def small_copy(step):
+        other = lax.rem(me + step, total)
+        return pltpu.make_async_remote_copy(
+            src_ref=small_own,
+            dst_ref=small_out.at[me],
+            send_sem=small_send.at[step - 1],
+            recv_sem=small_recv.at[me],
+            device_id={fs.name: lax.div(other, c_size), cx.name: lax.rem(other, c_size)},
+            device_id_type=pl.DeviceIdType.MESH,
+        )
+
+    def small_start(step, carry):
+        small_copy(step).start()
+        return carry
+
+    def small_wait(step, carry):
+        other = lax.rem(me + step, total)
+        arrived(small_out.at[other], small_recv.at[other])
+        return carry
+
+    def small_drain(step, carry):
+        small_copy(step).wait_send()
+        return carry
+
+    def vector(row, first, chunks, per):
+        parts = []
+        for chunk in range(chunks):
+            part = small_out[first + chunk * per, row : row + 1, :].astype(F32)
+            for more in range(1, per):
+                part = part + small_out[first + chunk * per + more, row : row + 1, :].astype(F32)
+            parts.append(part)
+        return jnp.concatenate(parts, axis=1)
+
+    def normalise():
+        width = acts[0].shape[1]
+        chunks = width // 128
+        gain = vector(0, 0, chunks, total // chunks)
+        shift = vector(1, 0, chunks, total // chunks)
+
+        def step(i, carry):
+            rows = pl.ds(pl.multiple_of(i * 32, 32), 32)
+            x = acts[0][rows, :].astype(F32)
+            centred = x - jnp.mean(x, axis=-1, keepdims=True)
+            inv_std = lax.rsqrt(jnp.mean(centred * centred, axis=-1, keepdims=True) + NORM_EPS)
+            act_outs[0][cx.me, rows, :] = (centred * inv_std * gain + shift).astype(BF16)
+            return carry
+
+        lax.fori_loop(0, acts[0].shape[0] // 32, step, 0)
+
+    def project():
+        rows, width = acts[0].shape
+        cols = query.shape[1]
+        per = total * cols // width
+        first = cx.me * per
+        bias = [vector(4 + part, first, cols // 128, per * 128 // cols) for part in range(3)]
+
+        def step(i, carry):
+            x = act_outs[0][pl.ds(2 * i, 2)].reshape(2 * rows, width)
+            span = pl.ds(pl.multiple_of(i * 2 * rows, 2 * rows), 2 * rows)
+            straight, swing = [table[span, :] for table in tables]
+            for part, out in enumerate((query, key, value)):
+                w = w_outs[0][:, :, :, part * cols : (part + 1) * cols].reshape(width, cols)
+                y = jnp.dot(x, w, preferred_element_type=F32) + bias[part]
+                for lane in range(0, cols, 128):
+                    half = y[:, lane : lane + 128]
+                    if part < 2:
+                        half = turn(half, straight, swing, 1.0)
+                    out[span, lane : lane + 128] = half.astype(BF16)
+            return carry
+
+        lax.fori_loop(0, c_size // 2, step, 0)
+
+    def attend(head):
+        length = query.shape[0]
+        block = math.gcd(length, 256)
+        lanes = slice(head * HEAD_DIM, (head + 1) * HEAD_DIM)
+        last_two = (((1,), (1,)), ((), ()))
+        for first in range(0, length, block):
+            last = first + block
+            scores = (
+                lax.dot_general(
+                    query[first:last, lanes],
+                    key[:last, lanes],
+                    last_two,
+                    preferred_element_type=F32,
+                )
+                * HEAD_DIM ** (-0.5)
+            )
+            row = lax.broadcasted_iota(jnp.int32, (block, last), 0) + first
+            col = lax.broadcasted_iota(jnp.int32, (block, last), 1)
+            scores = jnp.where(col <= row, scores, MASKED)
+            top = jnp.max(scores, axis=-1, keepdims=True)
+            weights = jnp.exp(scores - top)
+            summed = jnp.sum(weights, axis=-1, keepdims=True)
+            mixed = jnp.dot(weights.astype(BF16), value[:last, lanes], preferred_element_type=F32)
+            context[first:last, lanes] = (mixed / summed).astype(BF16)
+            lse[first:last, head : head + 1] = top + jnp.log(summed)
+
     meet_everyone(fs, cx)
-    own = []
-    for index in range(n_ctx):
-        copy = pltpu.make_async_copy(acts[index], lines[index].slot(cx.me), own_sem.at[index])
-        copy.start()
-        own.append(copy)
-    if small:
-        lines[n_act].start()
+    lax.fori_loop(1, total, small_start, 0)
     start_moves()
+    own = {}
+    small_own_copy = pltpu.make_async_copy(small_own, small_out.at[me], own_sem.at[n_act])
+    small_own_copy.start()
     for index in range(n_act):
-        lines[index].start()
+        if not (fused and index == 0):
+            own[index] = pltpu.make_async_copy(
+                acts[index], lines[index].slot(cx.me), own_sem.at[index]
+            )
+            own[index].start()
+            lines[index].start()
+    small_own_copy.wait()
+    lax.fori_loop(1, total, small_wait, 0)
+    if fused:
+        normalise()
+        lines[0].start()
+
     scatters = [functools.partial(start_scatter, index) for index in range(n_w)]
     starts = [functools.partial(start_spread, index) for index in range(n_w)]
     lasts = [functools.partial(forward_spread, index) for index in range(n_w)]
-    for work in scatters[:2]:
+    rows = [
+        [functools.partial(lines[index].forward, step) for step in range(1, cx.high)]
+        for index in range(n_act)
+    ]
+    comm = [scatters.pop(0)] + [more[0] for more in rows[1:]] + [scatters.pop(0), rows[0][0]]
+    comm += scatters
+    comm += rows[0][1:2] + [starts[0]] + [more[1] for more in rows[1:] if len(more) > 1]
+    comm += [starts[1], lasts[0]] + rows[0][2:]
+    for work in comm:
         work()
-    for step in range(1, cx.high):
-        if small:
-            lines[n_act].forward(step)
-        for index in range(n_act):
-            lines[index].forward(step)
-            if step == 1 and index == n_act - 1:
-                for work in scatters[2:]:
-                    work()
-            if starts and (step > 1 or index == n_act - 1):
-                starts.pop(0)()
-                if len(lasts) - len(starts) > 1:
-                    lasts.pop(0)()
-    for work in scatters[2:] if cx.high == 1 else []:
+    comm = []
+    for index in range(2, n_w):
+        comm += [starts[index], lasts[index - 1]]
+    comm += [work for more in rows[1:] for work in more[2:]] + [lasts[-1]]
+    lines[0].finish()
+    spreads[0].finish()
+    if fused:
+        compute = [project]
+        compute += [functools.partial(attend, head) for head in range(lse.shape[1])]
+        for work in compute:
+            if comm:
+                comm.pop(0)()
+            if comm and work is project:
+                comm.pop(0)()
+            work()
+    for work in comm:
         work()
-    while starts:
-        starts.pop(0)()
-        if len(lasts) - len(starts) > 1:
-            lasts.pop(0)()
-    for work in lasts:
-        work()
-    if small:
-        lines[n_act].finish()
-        own[n_act].wait()
-        small_spread.start()
-        for step in range(1, fs.high):
-            small_spread.forward(step)
-    for index in range(n_act):
+    for index in own:
         own[index].wait()
+    for index in range(1, n_act):
         lines[index].finish()
     for index in range(n_w):
-        spreads[index].finish()
+        if index > 0:
+            spreads[index].finish()
 
         @pl.when(jnp.logical_not(stays))
         def _(index=index):
@@ -369,34 +479,40 @@
             def _(away=away):
                 away().wait_send()
 
-    if small:
-        small_spread.finish()
-
-
-def gather_call(f_size, c_size, acts, w_srcs, small, collective_id):
+    lax.fori_loop(1, total, small_drain, 0)
+
+
+def gather_call(f_size, c_size, acts, small, w_srcs, tables, collective_id):
     ratio = c_size // f_size
-    ins = list(acts) + ([small] if small is not None else []) + list(w_srcs)
+    total = f_size * c_size
+    fused = tables is not None
+    ins = [*acts, small, *w_srcs] + (list(tables) if fused else [])
     shapes = [jax.ShapeDtypeStruct((c_size, *a.shape), a.dtype) for a in acts]
-    if small is not None:
-        shapes.append(jax.ShapeDtypeStruct((f_size, c_size, *small.shape), small.dtype))
+    shapes.append(jax.ShapeDtypeStruct((total, *small.shape), small.dtype))
     for w in w_srcs:
         shapes.append(jax.ShapeDtypeStruct((ratio, f_size, *w.shape[1:]), w.dtype))
-    n_ctx = len(acts) + (small is not None)
-    scratch = [pltpu.SemaphoreType.DMA((n_ctx,))]
-    for _ in range(n_ctx):
+    specs = [ANY] * len(shapes)
+    specs[len(acts)] = VMEM
+    if fused:
+        specs[0] = specs[len(acts) + 1] = VMEM
+        length, cols = c_size * acts[0].shape[0], w_srcs[0].shape[2] // 3
+        shapes += [jax.ShapeDtypeStruct((length, cols), BF16)] * 4
+        shapes.append(jax.ShapeDtypeStruct((length, cols // HEAD_DIM), F32))
+        specs += [VMEM] * 5
+    scratch = [pltpu.SemaphoreType.DMA((total - 1,)), pltpu.SemaphoreType.DMA((total,))]
+    scratch.append(pltpu.SemaphoreType.DMA((len(acts) + 1,)))
+    for _ in acts:
         scratch += line_sems(c_size)
     scratch += [pltpu.VMEM(w.shape, w.dtype) for w in w_srcs]
     scratch += [pltpu.SemaphoreType.DMA((len(w_srcs),))] * 2
     scratch += [pltpu.SemaphoreType.DMA((len(w_srcs), ratio))] * 2
-    for _ in range(len(w_srcs) + (small is not None)):
+    for _ in w_srcs:
         scratch += spread_sems(f_size)
     return pl.pallas_call(
-        functools.partial(
-            gather_kernel, len(acts), len(w_srcs), small is not None, f_size, c_size
-        ),
+        functools.partial(gather_kernel, len(acts), len(w_srcs), fused, f_size, c_size),
         out_shape=tuple(shapes),
         in_specs=[VMEM] * len(ins),
-        out_specs=tuple([ANY] * len(shapes)),
+        out_specs=tuple(specs),
         scratch_shapes=scratch,
         compiler_params=pltpu.CompilerParams(collective_id=collective_id, has_side_effects=True),
         name=f"gather_{collective_id}",
@@ -425,9 +541,9 @@
 
 
 class Fold:
-    def __init__(self, axis, block, result, from_lo, staged, from_hi, sems):
-        self.axis, self.block, self.result = axis, block, result
-        self.from_lo, self.staged, self.from_hi = from_lo, staged, from_hi
+    def __init__(self, axis, block, from_lo, from_hi, *sems):
+        self.axis, self.block, self.result = axis, block, from_lo.at[0]
+        self.from_lo, self.from_hi = from_lo, from_hi
         self.send_lo, self.recv_lo, self.send_hi, self.recv_hi = sems
 
     def copy_lo(self, step):
@@ -445,7 +561,7 @@
     def copy_hi(self, step):
         ax = self.axis
         return remote(
-            self.staged.at[step - 1],
+            self.from_lo.at[step],
             self.from_hi.at[step - 1],
             self.send_hi.at[step - 1],
             self.recv_hi.at[step - 1],
@@ -460,7 +576,7 @@
     def forward(self, step):
         arrived(self.from_lo.at[step], self.recv_lo.at[step])
         add_into(
-            self.staged.at[step - 1], [self.block(self.axis.ahead(step)), self.from_lo.at[step]]
+            self.from_lo.at[step], [self.block(self.axis.ahead(step)), self.from_lo.at[step]]
         )
         self.copy_hi(step).start()
 
@@ -480,8 +596,8 @@
 
 
 class LineFold:
-    def __init__(self, axis, block, result, from_lo, from_z, from_end, *sems):
-        self.axis, self.block, self.result = axis, block, result
+    def __init__(self, axis, block, own, result, from_lo, from_z, from_end, *sems):
+        self.axis, self.block, self.own, self.result = axis, block, own, result
         self.from_lo, self.from_z, self.from_end = from_lo, from_z, from_end
         self.send_lo, self.recv_lo, self.send_z, self.recv_z, self.recv_end = sems
         low_end, high_end = jnp.int32(0), jnp.int32(axis.high - 1)
@@ -521,7 +637,7 @@
     def pass_on(self, hi, up):
         ax = self.axis
         first = ax.hi == (0 if up else ax.high - 1)
-        own = self.block(ax.at(hi, ax.lo))
+        own = self.own(hi)
 
         @pl.when(first)
         def _():
@@ -556,7 +672,7 @@
 
     def finish(self):
         ax = self.axis
-        own = [self.block(ax.me), self.from_lo.at[ax.hi]]
+        own = [self.own(ax.hi), self.from_lo.at[ax.hi]]
         if ax.high == 1:
             add_into(self.result, own)
             return
@@ -612,7 +728,6 @@
     return [
         pltpu.VMEM((high, *shape), dtype),
         pltpu.VMEM((more, *shape), dtype),
-        pltpu.VMEM((more, *shape), dtype),
         pltpu.SemaphoreType.DMA((high,)),
         pltpu.SemaphoreType.DMA((high,)),
         pltpu.SemaphoreType.DMA((more,)),
@@ -620,33 +735,55 @@
     ]
 
 
-def reduce_kernel(n_part, n_w, f_size, c_size, *refs):
+def reduce_kernel(n_part, n_w, fused, f_size, c_size, *refs):
     fs, cx = Axis("fsdp", f_size), Axis("ctx", c_size)
     ratio = c_size // f_size
-    parts, refs = refs[:n_part], refs[n_part:]
-    grads, refs = refs[:n_w], refs[n_w:]
+    n_late = 1 if fused else 0
+    parts, refs = refs[: n_part - n_late], refs[n_part - n_late :]
+    grads, refs = refs[: n_w - n_late], refs[n_w - n_late :]
+    if fused:
+        heads_in, refs = refs[:6], refs[6:]
+        straight, swing, qkv_w, hidden, mlp_back = refs[:5]
+        refs = refs[5:]
     rows_outs, refs = refs[:n_part], refs[n_part:]
     grad_outs, scratch = refs[:n_w], list(refs[n_w:])
+    if fused:
+        sums = scratch.pop(0)
+        late_part, late_grad, own_rows, own_sem = scratch[:4]
+        dq, dk, dv, mixed_grad, tall, tall_sem, wide, wide_sem = scratch[4:12]
+        scratch = scratch[12:]
+        parts, grads = (*parts, late_part), (*grads, late_grad)
     row_folds = []
     for index in range(n_part):
         block = lambda c, part=parts[index]: part.at[c]
-        row_folds.append(LineFold(cx, block, rows_outs[index], *scratch[:8]))
+        own = lambda hi, block=block: block(cx.at(hi, cx.lo))
+        if fused and index == 0:
+            own = lambda hi: own_rows.at[hi]
+        row_folds.append(LineFold(cx, block, own, rows_outs[index], *scratch[:8]))
         scratch = scratch[8:]
     column = lax.div(cx.me, ratio)
     folds, totals = [], []
     for index in range(n_w):
-        grad = grads[index]
-        block = lambda f, grad=grad: grad.at[:, low_slot(fs, column, f)]
-        totals.append(scratch[7])
-        folds.append(Fold(fs, block, scratch[7], *scratch[:3], scratch[3:7]))
-        scratch = scratch[8:]
+        block = lambda f, grad=grads[index]: grad.at[:, low_slot(fs, column, f)]
+        totals.append(scratch[0].at[0])
+        folds.append(Fold(fs, block, *scratch[:6]))
+        scratch = scratch[6:]
     g_send, g_recv = scratch
 
     meet_everyone(fs, cx)
-    for fold in row_folds:
+    for fold in row_folds[: n_part - n_late]:
         fold.start()
-    for fold in folds:
+    for fold in folds[: n_w - n_late]:
         fold.start()
+    own_copies = []
+    if fused:
+        for hi in range(cx.high):
+            own_copies.append(
+                pltpu.make_async_copy(
+                    parts[0].at[cx.at(hi, cx.lo)], own_rows.at[hi], own_sem.at[hi]
+                )
+            )
+            own_copies[-1].start()
 
     slot = lax.rem(cx.me, ratio)
     row_lo = low_slot(fs, column, fs.me)
@@ -684,19 +821,109 @@
         for step in range(1, fs.high):
             folds[index].forward(step)
 
-    row_work = [
-        functools.partial(fold.forward, hi) for fold in row_folds for hi in fold.order
-    ]
+    def row_work(fold):
+        return [functools.partial(fold.forward, hi) for hi in fold.order]
+
     halves = [functools.partial(pass_halves, index) for index in range(n_w)]
     delivers = [functools.partial(deliver_all, index) for index in range(n_w)]
-    for count, work in enumerate(row_work):
-        for more in halves[:2]:
-            more()
-        halves = halves[2:]
-        work()
-        if count >= 1 and delivers and not halves:
-            delivers.pop(0)()
-    for work in halves + delivers:
+
+    def column_grads():
+        wide_rows = late_grad.shape[2]
+
+        def copy(i):
+            at = pl.ds(pl.multiple_of(i * wide_rows, wide_rows), wide_rows)
+            slot = lax.rem(i, 2)
+            return pltpu.make_async_copy(hidden.at[:, at], tall.at[slot], tall_sem.at[slot])
+
+        copy(0).start()
+
+        def step(i, carry):
+            @pl.when(i + 1 < c_size)
+            def _():
+                copy(i + 1).start()
+
+            copy(i).wait()
+            late_grad[lax.div(i, f_size), lax.rem(i, f_size)] = lax.dot_general(
+                tall[lax.rem(i, 2)],
+                mixed_grad[...],
+                (((0,), (0,)), ((), ())),
+                preferred_element_type=F32,
+            ).astype(BF16)
+            return carry
+
+        lax.fori_loop(0, c_size, step, 0)
+
+    def row_grads():
+        rows = late_part.shape[1]
+
+        def copy(i):
+            slot = lax.rem(i, 2)
+            return pltpu.make_async_copy(
+                mlp_back.at[pl.ds(2 * i, 2)], wide.at[slot], wide_sem.at[slot]
+            )
+
+        copy(0).start()
+
+        def step(i, carry):
+            @pl.when(i + 1 < c_size // 2)
+            def _():
+                copy(i + 1).start()
+
+            copy(i).wait()
+            span = pl.ds(pl.multiple_of(2 * i * rows, 2 * rows), 2 * rows)
+            total = lax.dot_general(
+                mixed_grad[span, :],
+                qkv_w[...],
+                (((1,), (1,)), ((), ())),
+                preferred_element_type=F32,
+            )
+            total = total.reshape(2, rows, total.shape[1]) + wide[lax.rem(i, 2)]
+            late_part[pl.ds(2 * i, 2)] = total.astype(BF16)
+            return carry
+
+        lax.fori_loop(0, c_size // 2, step, 0)
+
+    if fused:
+        heads = dq.shape[1] // HEAD_DIM
+        early = row_work(row_folds[0])
+        comm = [early.pop(0), early.pop(0), delivers.pop(0)]
+        for work in early:
+            comm.append(work)
+            if len(delivers) > 1:
+                comm.append(delivers.pop(0))
+        for work in halves[:-1]:
+            work()
+        for copy in own_copies:
+            copy.wait()
+        for head in range(heads):
+            backward_head(head, *heads_in, dq, dk, dv)
+            if comm:
+                comm.pop(0)()
+        backward_turn(straight, swing, dq, dk, dv, mixed_grad, sums)
+        row_grads()
+        row_folds[1].start()
+        if comm:
+            comm.pop(0)()
+        column_grads()
+        folds[-1].start()
+        for work in comm:
+            work()
+        halves[-1]()
+        for count, work in enumerate(row_work(row_folds[1])):
+            work()
+            if count >= 1 and delivers:
+                delivers.pop(0)()
+    else:
+        for count, work in enumerate([work for fold in row_folds for work in row_work(fold)]):
+            for more in halves[:2]:
+                more()
+            halves = halves[2:]
+            work()
+            if count >= 1 and delivers and not halves:
+                delivers.pop(0)()
+        for work in halves:
+            work()
+    for work in delivers:
         work()
     for fold in row_folds:
         fold.finish()
@@ -715,37 +942,77 @@
                 away().wait_send()
 
 
-def reduce_call(f_size, c_size, parts, grads, collective_id):
+def reduce_call(f_size, c_size, parts, grads, collective_id, late=None):
     ratio = c_size // f_size
+    fused = late is not None
+    ins, in_specs = [*parts, *grads], [VMEM] * (len(parts) + len(grads))
+    part_shapes = [(part.shape, part.dtype) for part in parts]
+    grad_shapes = [(grad.shape, grad.dtype) for grad in grads]
+    own = []
+    if fused:
+        in_specs[0] = ANY
+        heads_in, tables, qkv_w, hidden, mlp_back = late
+        ins += [*heads_in, *tables, qkv_w, hidden, mlp_back]
+        in_specs += [VMEM] * 9 + [ANY] * 2
+        length, cols = heads_in[0].shape
+        part_shapes.append(part_shapes[0])
+        shape, dtype = grad_shapes[0]
+        grad_shapes.append(((*shape[:3], 3 * cols), dtype))
+        high = c_size // LOW
+        own = [
+            pltpu.VMEM(*part_shapes[1]),
+            pltpu.VMEM(*grad_shapes[-1]),
+            pltpu.VMEM((high, *parts[0].shape[1:]), BF16),
+            pltpu.SemaphoreType.DMA((high,)),
+            pltpu.VMEM((length, cols), F32),
+            pltpu.VMEM((length, cols), F32),
+            pltpu.VMEM((length, cols), F32),
+            pltpu.VMEM((length, 3 * cols), BF16),
+            pltpu.VMEM((2, length, shape[2]), BF16),
+            pltpu.SemaphoreType.DMA((2,)),
+            pltpu.VMEM((2, 2, *mlp_back.shape[1:]), F32),
+            pltpu.SemaphoreType.DMA((2,)),
+        ]
     shapes, scratch = [], []
-    for part in parts:
-        shapes.append(jax.ShapeDtypeStruct(part.shape[1:], F32))
-        scratch += line_fold_scratch(c_size, part.shape[1:], part.dtype)
-    for g in grads:
-        piece = (ratio, *g.shape[2:])
-        shapes.append(jax.ShapeDtypeStruct(piece, g.dtype))
-        scratch += fold_scratch(f_size, piece, g.dtype) + [pltpu.VMEM(piece, g.dtype)]
-    scratch += [pltpu.SemaphoreType.DMA((len(grads), ratio))] * 2
+    for shape, dtype in part_shapes:
+        shapes.append(jax.ShapeDtypeStruct(shape[1:], F32))
+        scratch += line_fold_scratch(c_size, shape[1:], dtype)
+    for shape, dtype in grad_shapes:
+        piece = (ratio, *shape[2:])
+        shapes.append(jax.ShapeDtypeStruct(piece, dtype))
+        scratch += fold_scratch(f_size, piece, dtype)
+    specs = [VMEM] * len(part_shapes) + [ANY] * len(grad_shapes)
+    if fused:
+        shapes.append(jax.ShapeDtypeStruct((1, 3 * cols), F32))
+        specs.append(VMEM)
+    scratch += [pltpu.SemaphoreType.DMA((len(grad_shapes), ratio))] * 2
     outs = pl.pallas_call(
-        functools.partial(reduce_kernel, len(parts), len(grads), f_size, c_size),
+        functools.partial(
+            reduce_kernel, len(part_shapes), len(grad_shapes), fused, f_size, c_size
+        ),
         out_shape=tuple(shapes),
-        in_specs=[VMEM] * (len(parts) + len(grads)),
-        out_specs=tuple([VMEM] * len(shapes)),
-        scratch_shapes=scratch,
-        compiler_params=pltpu.CompilerParams(collective_id=collective_id, has_side_effects=True),
+        in_specs=in_specs,
+        out_specs=tuple(specs),
+        scratch_shapes=own + scratch,
+        compiler_params=pltpu.CompilerParams(
+            collective_id=collective_id,
+            has_side_effects=True,
+            vmem_limit_bytes=66_000_000 if fused else None,
+        ),
         name=f"reduce_{collective_id}",
-    )(*parts, *grads)
-    return outs[: len(parts)], outs[len(parts) :]
+    )(*ins)
+    n_part, n_w = len(part_shapes), len(grad_shapes)
+    return outs[:n_part], outs[n_part : n_part + n_w], outs[n_part + n_w :]
 
 
 def reduce_all(f_size, c_size, parts, grads):
     size = sum(2.25 * part.size * part.dtype.itemsize for part in parts)
     size += sum(2.5 * grad.size * grad.dtype.itemsize for grad in grads)
     if size <= 56 * 2**20:
-        return reduce_call(f_size, c_size, parts, grads, 2)
+        return reduce_call(f_size, c_size, parts, grads, 2)[:2]
     half = len(grads) // 2
-    (first,), early = reduce_call(f_size, c_size, parts[:1], grads[:half], 2)
-    (second,), late = reduce_call(f_size, c_size, parts[1:], grads[half:], 3)
+    (first,), early, _ = reduce_call(f_size, c_size, parts[:1], grads[:half], 2)
+    (second,), late, _ = reduce_call(f_size, c_size, parts[1:], grads[half:], 3)
     return (first, second), (*early, *late)
 
 
@@ -837,6 +1104,81 @@
         ],
         axis=-1,
     )
+
+
+def lane_tables(count):
+    half_dim = ROT_DIM // 2
+    inverse = np.float32(10000.0) ** (-(np.arange(half_dim, dtype=np.float32) * 2.0) / ROT_DIM)
+    angles = np.arange(count, dtype=np.float32)[:, None] * inverse.astype(np.float32)[None, :]
+    cosine, sine = np.cos(angles.astype(np.float64)), np.sin(angles.astype(np.float64))
+    rest = np.zeros((count, HEAD_DIM - ROT_DIM))
+    straight = np.concatenate([cosine, cosine, rest + 1.0] * (128 // HEAD_DIM), axis=1)
+    swing = np.concatenate([-sine, sine, rest] * (128 // HEAD_DIM), axis=1)
+    return [jnp.asarray(table.astype(np.float32)) for table in (straight, swing)]
+
+
+def turn(values, straight, swing, sign):
+    half_dim = ROT_DIM // 2
+    lane = lax.broadcasted_iota(jnp.int32, values.shape, 1)
+    first = lax.rem(lane, HEAD_DIM) < half_dim
+    other = jnp.where(
+        first, pltpu.roll(values, 128 - half_dim, 1), pltpu.roll(values, half_dim, 1)
+    )
+    return values * straight + sign * other * swing
+
+
+def backward_head(head, query, key, value, context, context_grad, lse, dq, dk, dv):
+    length = query.shape[0]
+    block = math.gcd(length, 256)
+    scale = HEAD_DIM ** (-0.5)
+    last_two = (((1,), (1,)), ((), ()))
+    first_two = (((0,), (0,)), ((), ()))
+
+    def dot(left, right, dims):
+        return lax.dot_general(left, right, dims, preferred_element_type=F32)
+
+    lanes = slice(head * HEAD_DIM, (head + 1) * HEAD_DIM)
+    for first in reversed(range(0, length, block)):
+        last = first + block
+        q, g = query[first:last, lanes], context_grad[first:last, lanes]
+        k, v = key[:last, lanes], value[:last, lanes]
+        delta = jnp.sum(
+            g.astype(F32) * context[first:last, lanes].astype(F32), axis=-1, keepdims=True
+        )
+        scores = dot(q, k, last_two) * scale
+        row = lax.broadcasted_iota(jnp.int32, (block, last), 0) + first
+        col = lax.broadcasted_iota(jnp.int32, (block, last), 1)
+        probs = jnp.where(col <= row, jnp.exp(scores - lse[first:last, head : head + 1]), 0.0)
+        score_grad = (probs * (dot(g, v, last_two) - delta)).astype(BF16)
+        value_grad = dot(probs.astype(BF16), g, first_two)
+        key_grad = dot(score_grad, q, first_two) * scale
+        dq[first:last, lanes] = dot(score_grad, k, (((1,), (0,)), ((), ()))) * scale
+        if last == length:
+            dv[:, lanes] = value_grad
+            dk[:, lanes] = key_grad
+        else:
+            dv[:last, lanes] += value_grad
+            dk[:last, lanes] += key_grad
+
+
+def backward_turn(straight, swing, dq, dk, dv, out, sums):
+    length, cols = dq.shape
+    block = math.gcd(length, 256)
+    for part, grad in enumerate((dq, dk, dv)):
+        for lane in range(0, cols, 128):
+            at = part * cols + lane
+
+            def step(i, total, grad=grad, lane=lane, at=at, part=part):
+                rows = pl.ds(pl.multiple_of(i * block, block), block)
+                values = grad[rows, lane : lane + 128]
+                if part < 2:
+                    values = turn(values, straight[rows, :], swing[rows, :], -1.0)
+                out[rows, at : at + 128] = values.astype(BF16)
+                return total + jnp.sum(values, axis=0, keepdims=True)
+
+            sums[:, at : at + 128] = lax.fori_loop(
+                0, length // block, step, jnp.zeros((1, 128), F32)
+            )
 
 
 def attention_forward(query, key, value, scale):
@@ -919,15 +1261,20 @@
 
     vec = norm_gain.shape[0]
     vec1 = fc1_bias.shape[0]
+    me = lax.axis_index("fsdp") * c_size + c_index
+    per = max(128 // vec, 1)
+    lane_piece = jnp.arange(128) // vec == me % per
+
+    def placed(vector):
+        return jnp.where(lane_piece, jnp.tile(vector.reshape(-1, vec), (1, per)), 0).astype(BF16)
+
     def lanes(array):
         array = array.reshape(-1, min(array.shape[-1], 128))
         return jnp.pad(array, ((0, 0), (0, 128 - array.shape[1])))
 
     small = jnp.concatenate(
-        [
-            lanes(v)
-            for v in (norm_gain, norm_bias, out_bias, fc2_bias, qkv_bias, fc1_bias)
-        ]
+        [placed(v) for v in (norm_gain, norm_bias, out_bias, fc2_bias, qkv_bias)]
+        + [lanes(fc1_bias)]
     )
     small = jnp.pad(small, ((0, -small.shape[0] % 16), (0, 0)))
 
@@ -939,14 +1286,18 @@
     out_src = jnp.transpose(out_weight.reshape(ratio, cols, row_block), (0, 2, 1))
     fc2_src = jnp.transpose(fc2_weight.reshape(ratio, hidden_cols, row_block), (0, 2, 1))
 
-    tok_all, cot_all, small_all, qkv_all, fc1_all, fc2_all, out_all = gather_call(
+    fused = cols % 128 == 0 and row_block % 128 == 0 and own_seqs == 1
+    tables = lane_tables(length) if fused else None
+    gathered = gather_call(
         f_size,
         c_size,
         [tokens.reshape(own_rows, width), cotangent.reshape(own_rows, width)],
+        small,
         [qkv_src, fc1_src, fc2_src, out_src],
-        small,
+        tables,
         0,
     )
+    first_all, cot_all, small_all, qkv_all, fc1_all, fc2_all, out_all = gathered[:7]
 
     def rows_of(gathered):
         return jnp.swapaxes(gathered.reshape(c_size, own_seqs, tok_count, width), 0, 1).reshape(
@@ -958,7 +1309,6 @@
             c_size, own_rows, width
         )
 
-    x_rows = rows_of(tok_all)
     grad_rows = rows_of(cot_all)
     qkv_w = qkv_all.reshape(width, 3 * cols)
     fc1_w = fc1_all.reshape(width, hidden_cols)
@@ -966,36 +1316,36 @@
     fc2_t = fc2_all.reshape(width, hidden_cols)
 
     vectors = small_all.reshape(devices, -1, 128)
-    gain_full = vectors[:, 0, :vec].reshape(-1).astype(F32)
-    shift_full = vectors[:, 1, :vec].reshape(-1).astype(F32)
-    out_bias_full = vectors[:, 2, :vec].reshape(-1).astype(F32)
-    fc2_bias_full = vectors[:, 3, :vec].reshape(-1).astype(F32)
-    qkv_bias_full = jnp.swapaxes(vectors[:, 4:7, :vec], 0, 1).reshape(3, -1)
+    joined = jnp.sum(vectors[:, :7].astype(F32).reshape(devices // per, per, 7, 128), axis=1)
+    joined = jnp.swapaxes(joined, 0, 1).reshape(7, width)
+    gain_full, shift_full, out_bias_full, fc2_bias_full = (joined[i] for i in range(4))
     lane = min(vec1, 128)
     fc1_bias_full = vectors[:, 7 : 7 + vec1 // lane, :lane].reshape(-1)
-    qkv_b = (
-        lax.dynamic_slice_in_dim(qkv_bias_full, c_index * cols, cols, 1).reshape(-1).astype(F32)
-    )
     fc1_b = lax.dynamic_slice_in_dim(fc1_bias_full, c_index * hidden_cols, hidden_cols, 0).astype(
         F32
     )
 
-    normed, _ = normed_of(x_rows.astype(F32))
-    hidden_in = (normed * gain_full + shift_full).astype(BF16)
-    mixed = jnp.dot(hidden_in, qkv_w, preferred_element_type=F32) + qkv_b
-    cosine, sine = rope_tables(length, ROT_DIM)
-
     def heads_of(array):
         return array.reshape(own_seqs, length, heads, head_dim)
 
-    query = rotate_pairs(heads_of(mixed[:, :cols]), cosine, sine, ROT_DIM, 1.0).astype(BF16)
-    key = rotate_pairs(heads_of(mixed[:, cols : 2 * cols]), cosine, sine, ROT_DIM, 1.0).astype(
-        BF16
-    )
-    value = heads_of(mixed[:, 2 * cols :].astype(BF16))
-    forward = [attention_forward(query[s], key[s], value[s], scale) for s in range(own_seqs)]
-    context_b = jnp.stack([pair[0] for pair in forward]).astype(BF16)
-    context_rows = context_b.reshape(rows, cols)
+    if fused:
+        hidden_in = rows_of(first_all)
+        context_rows = gathered[10]
+    else:
+        cosine, sine = rope_tables(length, ROT_DIM)
+        qkv_b = lax.dynamic_slice_in_dim(joined[4:7], c_index * cols, cols, 1).reshape(-1)
+        normed, _ = normed_of(rows_of(first_all).astype(F32))
+        hidden_in = (normed * gain_full + shift_full).astype(BF16)
+        mixed = jnp.dot(hidden_in, qkv_w, preferred_element_type=F32) + qkv_b
+        query, key = (
+            rotate_pairs(heads_of(part), cosine, sine, ROT_DIM, 1.0).astype(BF16)
+            for part in (mixed[:, :cols], mixed[:, cols : 2 * cols])
+        )
+        value = heads_of(mixed[:, 2 * cols :].astype(BF16))
+        forward = [attention_forward(query[s], key[s], value[s], scale) for s in range(own_seqs)]
+        context_b = jnp.stack([pair[0] for pair in forward]).astype(BF16)
+        lse = jnp.stack([pair[1] for pair in forward])
+        context_rows = context_b.reshape(rows, cols)
     pre = jnp.dot(hidden_in, fc1_w, preferred_element_type=F32) + fc1_b
     act, slope = gelu_both(pre)
     act_b = act.astype(BF16)
@@ -1017,37 +1367,58 @@
     out_grad = weight_grad(grad_rows, context_rows)
     fc1_b_grad = jnp.sum(pre_grad, axis=0)
     mlp_back = lax.dot_general(pre_grad_b, fc1_w, contract_last, preferred_element_type=F32)
-    context_grad = heads_of(jnp.dot(grad_rows, out_t, preferred_element_type=F32).astype(BF16))
-    delta = jnp.swapaxes(
-        jnp.sum(context_grad.astype(F32) * context_b.astype(F32), axis=-1), 1, 2
-    )
-    grads = [
-        attention_backward(
-            query[s], key[s], value[s], context_grad[s], delta[s], forward[s][1], scale
-        )
-        for s in range(own_seqs)
-    ]
-    query_grad, key_grad, value_grad = [jnp.stack(parts) for parts in zip(*grads)]
-    mixed_grad = jnp.concatenate(
-        [
-            rotate_pairs(query_grad, cosine, sine, ROT_DIM, -1.0).reshape(rows, cols),
-            rotate_pairs(key_grad, cosine, sine, ROT_DIM, -1.0).reshape(rows, cols),
-            value_grad.reshape(rows, cols),
-        ],
-        axis=1,
-    )
-    mixed_grad_b = mixed_grad.astype(BF16)
-    qkv_grad = weight_grad(hidden_in, mixed_grad_b)
-    qkv_b_grad = jnp.sum(mixed_grad, axis=0).reshape(3, cols)
-    normed_part = (
-        lax.dot_general(mixed_grad_b, qkv_w, contract_last, preferred_element_type=F32) + mlp_back
-    )
-    (branch, normed_grad), (fc2_shard, fc1_shard, out_shard, qkv_shard) = reduce_all(
-        f_size,
-        c_size,
-        [blocks_of(partial_out.astype(BF16)), blocks_of(normed_part.astype(BF16))],
-        [fc2_grad, fc1_grad, out_grad, qkv_grad],
-    )
+    context_grad = jnp.dot(grad_rows, out_t, preferred_element_type=F32).astype(BF16)
+    out_blocks = blocks_of(partial_out.astype(BF16))
+    if fused:
+        (branch, normed_grad), (fc2_shard, fc1_shard, out_shard, qkv_shard), (sums_qkv,) = (
+            reduce_call(
+                f_size,
+                c_size,
+                [out_blocks],
+                [fc2_grad, fc1_grad, out_grad],
+                2,
+                (
+                    [*gathered[7:11], context_grad, gathered[11]],
+                    tables,
+                    qkv_w,
+                    hidden_in,
+                    blocks_of(mlp_back),
+                ),
+            )
+        )
+        qkv_b_grad = sums_qkv.reshape(3, cols)
+    else:
+        context_grad = heads_of(context_grad)
+        delta = jnp.swapaxes(
+            jnp.sum(context_grad.astype(F32) * context_b.astype(F32), axis=-1), 1, 2
+        )
+        grads = [
+            attention_backward(
+                query[s], key[s], value[s], context_grad[s], delta[s], lse[s], scale
+            )
+            for s in range(own_seqs)
+        ]
+        query_grad, key_grad, value_grad = [jnp.stack(parts) for parts in zip(*grads)]
+        mixed_grad = jnp.concatenate(
+            [
+                rotate_pairs(query_grad, cosine, sine, ROT_DIM, -1.0).reshape(rows, cols),
+                rotate_pairs(key_grad, cosine, sine, ROT_DIM, -1.0).reshape(rows, cols),
+                value_grad.reshape(rows, cols),
+            ],
+            axis=1,
+        )
+        mixed_grad_b = mixed_grad.astype(BF16)
+        qkv_b_grad = jnp.sum(mixed_grad, axis=0).reshape(3, cols)
+        qkv_grad = weight_grad(hidden_in, mixed_grad_b)
+        normed_part = (
+            lax.dot_general(mixed_grad_b, qkv_w, contract_last, preferred_element_type=F32) + mlp_back
+        )
+        (branch, normed_grad), (fc2_shard, fc1_shard, out_shard, qkv_shard) = reduce_all(
+            f_size,
+            c_size,
+            [out_blocks, blocks_of(normed_part.astype(BF16))],
+            [fc2_grad, fc1_grad, out_grad, qkv_grad],
+        )
 
     x_own = tokens.reshape(own_rows, width).astype(F32)
     cot_own = cotangent.reshape(own_rows, width).astype(F32)

time: 490 us -> 471 us (0.961)
  matrix products: 86.5 us -> 50.1 us
  Pallas kernels: 341 us -> 367 us
  other arithmetic: 24.6 us -> 11.5 us
    dot_general x26 -> x0, matrix products: 29.4 us -> none  [the longest x1 6.45 us: body(): mixed = jnp.dot(hidden_in, qkv_w, preferred_element_type=F32) + qkv_b]
    pallas_call x2, Pallas kernels: 317 us -> 343 us  [the longest x1 195 us: gather_call(): pl.pallas_call(functools.partial(gather_kernel, len(acts), len(w_srcs), f...]
    convert_element_type x4 -> x0, other arithmetic: 7.15 us -> none  [the longest x2 6.4 us: body(): hidden_in = (normed * gain_full + shift_full).astype(BF16)]
    unnamed x78 -> x41, local copies, waits for them, and re-layouts: 11.5 us -> 9.16 us
    dot_general x4 -> x3, matrix products: 20.4 us -> 19.1 us  [weight_grad(): lax.dot_general(left, right, contract_first, preferred_element_type=F32)]
where the time goes in v3:
time: 471 us; the launch traced here: 462 us
  Pallas kernels  367 us (78%)
  matrix products  50.1 us (11%)
  local copies, waits for them, and re-layouts  32.1 us (7%)
  other arithmetic  11.5 us (2%)
    pallas_call x1, Pallas kernels, gather_call(): pl.pallas_call(functools.partial(gather_kernel, len(acts), len(w_srcs), f...  195 us
    pallas_call x1, Pallas kernels, reduce_call(): pl.pallas_call(functools.partial(reduce_kernel, len(part_shapes), len(gra...  148 us
    pallas_call x1, Pallas kernels, small_call(): pl.pallas_call(functools.partial(small_kernel, f_size, c_size), out_shape...  24.1 us
    dot_general x3, matrix products, weight_grad(): lax.dot_general(left, right, contract_first, preferred_element_type=F32)  19.1 us

profile of v3, /device:TPU:0, one launch (start us, length us, event | category | flops | bytes accessed | tf_op | source)
XLA Modules:
  0.0 462.2 jit_solution(15667594151224061067)
XLA Ops:
  3.8 1.2 convert_reduce_fusion
  5.0 1.3 fusion.15
  8.5 1.8 copy.44
  10.3 1.4 copy.39
  11.7 1.2 copy.45.refs_3_
  13.4 1.3 copy.42
  14.7 2.3 copy.43
  17.0 194.9 %gather_0.1 = (bf16[8,128,2048]{2,1,0:T(8,128)(2,1)}, bf16[8,128,2048]{2,1,0:T(8,128)(2,1)}, bf16[32,16,128]{2,1,0:T(8,128)(2,1)}, bf16[2,4,256,768]{3,2,1,0:T(8...) custom-call(bf16[128,2048]{1,0:T(8,128)(2,1)} %bitcast.83, ...), custom_call_target="tpu_custom_call" | custom-call | tf_op jit(solution)/shard_map/gather_0/pallas_call | solution.py:511
  211.9 1.1 slice.40
  213.0 1.2 convert_reduce_fusion.2
  214.3 4.5 convolution_convert_fusion.3.refs_8_
  218.8 2.4 convolution_convert_fusion.2
  221.2 1.5 copy-done.10
  222.7 4.5 fusion.28
  227.2 7.0 %fusion.25 = (f32[1024]{0:T(1024)S(1)}, bf16[1024,1024]{1,0:T(8,128)(2,1)S(1)}) fusion(f32[1024,1024]{1,0:T(8,128)S(1)} %fusion.28, f32[1024]{0:T(1024)S(1)} %dynamic-slice_convert_fusion, bf16[1024,2048]{1,0:T(8,128)(2,1)S(1)} %bitcast.124, bf16[2048,1024]{1,0:T(8,128)(2,1)S(1)} %bitcast.119), kind=kOutput, calls=%fused_computation.64 | convolution fusion | flops 4316986368 | bytes 14688256 | tf_op jit(solution)/shard_map/dot_general | solution.py:1357
  234.7 10.3 %convolution_convert_fusion.1 = bf16[2048,1024]{1,0:T(8,128)(2,1)} fusion(bf16[1024,2048]{1,0:T(8,128)(2,1)} %bitcast.122, f32[1024,1024]{1,0:T(8,128)} %copy-done.15, f32[1024]{0:T(1024)S(1)} %dynamic-slice_convert_fusion), kind=kOutput, calls=%fused_computation.11 | convolution fusion | flops 4307550208 | bytes 12587008 | tf_op jit(solution)/shard_map/dot_general | solution.py:1362
  245.0 4.9 %fusion.24 = f32[1024,2048]{1,0:T(8,128)S(1)} fusion(bf16[2048,1024]{1,0:T(8,128)(2,1)S(1)} %bitcast.120, f32[1024,1024]{1,0:T(8,128)S(1)} %copy-done.16, f32[1024]{0:T(1024)S(1)} %dynamic-slice_convert_fusion), kind=kOutput, calls=%fused_computation.63 | convolution fusion | flops 4305453056 | bytes 16781312 | tf_op jit(solution)/shard_map/dot_general | solution.py:1355
  250.0 3.2 add_convert_fusion
  253.2 6.8 %fusion.29.refs_14_ = f32[8,128,2048]{2,1,0:T(8,128)} fusion(bf16[8,128,1024]{2,1,0:T(8,128)(2,1)S(1)} %bitcast.125, bf16[2048,1024,1]{1,0,2:T(8,128)(2,1)S(1)} %bitcast.118), kind=kOutput, calls=%fused_computation.68 | convolution fusion | flops 4294967296 | bytes 14680064 | tf_op jit(solution)/shard_map/dot_general | solution.py:1369
  260.0 6.4 %convolution_convert_fusion = bf16[2048,1024]{1,0:T(8,128)(2,1)} fusion(bf16[1024,2048]{1,0:T(8,128)(2,1)S(1)} %bitcast.92, bf16[1024,1024]{1,0:T(8,128)(2,1)S(1)} %get-tuple-element.79), kind=kOutput, calls=%fused_computation.10 | convolution fusion | flops 4297064448 | bytes 10485760 | tf_op jit(solution)/shard_map/dot_general | solution.py:1362
  266.4 148.1 %reduce_2.1 = (f32[128,2048]{1,0:T(8,128)}, f32[128,2048]{1,0:T(8,128)}, bf16[2,256,1024]{2,1,0:T(8,128)(2,1)}, bf16[2,256,1024]{2,1,0:T(8,128)(2,1)}, bf16[2,25...) custom-call(bf16[8,128,2048]{2,1,0:T(8,128)(2,1)} %bitcast.82, ...), custom_call_target="tpu_custom_call" | custom-call | tf_op jit(solution)/shard_map/reduce_2/pallas_call | solution.py:989
  415.6 1.8 fusion.14
  417.4 3.5 convert_reduce_fusion.1
  421.9 24.1 %small_4.1 = f32[8,128]{1,0:T(8,128)} custom-call(f32[32,8,128]{2,1,0:T(8,128)} %bitcast.106), custom_call_target="tpu_custom_call" | custom-call | tf_op jit(solution)/shard_map/small_4/pallas_call | solution.py:1057
  445.9 1.2 slice_bitcast_fusion
  447.2 1.4 fusion.27
  449.9 1.0 copy.49
  451.3 1.6 copy.52
  453.0 1.5 convert_bitcast_fusion.1
  454.4 1.8 copy.50
  456.3 2.9 copy.53
  459.4 1.8 copy.51
  (80 shorter events, 11.0 us)
Async XLA Ops:
  0.6 12.3 %copy-start.6 = (bf16[256,2048]{1,0:T(8,128)(2,1)S(1)}, bf16[256,2048]{1,0:T(8,128)(2,1)}, u32[]{:S(2)}) copy-start(bf16[256,2048]{1,0:T(8,128)(2,1)} %param.21) | copy-start | bytes 3145732
  211.9 6.9 %copy-start.3 = (bf16[1024,256]{1,0:T(8,128)(2,1)S(1)}, bf16[1024,256]{1,0:T(8,128)(2,1)}, u32[]{:S(2)}) copy-start(bf16[1024,256]{1,0:T(8,128)(2,1)} %get-tuple-element.31.refs_7_) | copy-start | bytes 1572868
  211.9 6.9 %copy-start.14 = (bf16[8,128,2048]{2,1,0:T(8,128)(2,1)S(1)}, bf16[8,128,2048]{2,1,0:T(8,128)(2,1)}, u32[]{:S(2)}) copy-start(bf16[8,128,2048]{2,1,0:T(8,128)(2,1)} %get-tuple-element.37) | copy-start | bytes 12582916
  218.8 2.4 copy-start.1
  218.8 3.8 copy-start.10
  222.7 4.5 copy-start.12
  227.2 7.0 %copy-start.15 = (f32[1024,1024]{1,0:T(8,128)}, f32[1024,1024]{1,0:T(8,128)S(1)}, u32[]{:S(2)}) copy-start(f32[1024,1024]{1,0:T(8,128)S(1)} %fusion.28) | copy-start | bytes 12582916
  234.7 10.3 %copy-start.13 = (bf16[2,4,256,1024]{3,2,1,0:T(8,128)(2,1)S(1)}, bf16[2,4,256,1024]{3,2,1,0:T(8,128)(2,1)}, u32[]{:S(2)}) copy-start(bf16[2,4,256,1024]{3,2,1,0:T(8,128)(2,1)} %get-tuple-element.36) | copy-start | bytes 12582916
  234.7 10.3 %copy-start.16 = (f32[1024,1024]{1,0:T(8,128)S(1)}, f32[1024,1024]{1,0:T(8,128)}, u32[]{:S(2)}) copy-start(f32[1024,1024]{1,0:T(8,128)} %copy-done.15) | copy-start | bytes 12582916
  245.0 4.9 %copy-start.5 = (bf16[2,4,256,256]{3,2,1,0:T(8,128)(2,1)S(1)}, bf16[2,4,256,256]{3,2,1,0:T(8,128)(2,1)}, u32[]{:S(2)}) copy-start(bf16[2,4,256,256]{3,2,1,0:T(8,128)(2,1)} %get-tuple-element.32) | copy-start | bytes 3145732
  249.9 3.2 copy-start.11
  253.2 6.8 %copy-start.2 = (bf16[8,128,2048]{2,1,0:T(8,128)(2,1)S(1)}, bf16[8,128,2048]{2,1,0:T(8,128)(2,1)}, u32[]{:S(2)}) copy-start(bf16[8,128,2048]{2,1,0:T(8,128)(2,1)} %get-tuple-element.33) | copy-start | bytes 12582916
  266.4 149.1 %copy-start = (bf16[1,128,2048]{2,1,0:T(8,128)(2,1)S(1)}, bf16[1,128,2048]{2,1,0:T(8,128)(2,1)}, u32[]{:S(2)}) copy-start(bf16[1,128,2048]{2,1,0:T(8,128)(2,1)} %param.14) | copy-start | bytes 1572868
  414.6 35.3 %copy-start.8 = (bf16[2,256,256]{2,1,0:T(8,128)(2,1)S(1)}, bf16[2,256,256]{2,1,0:T(8,128)(2,1)}, u32[]{:S(2)}) copy-start(bf16[2,256,256]{2,1,0:T(8,128)(2,1)} %get-tuple-element.47) | copy-start | bytes 786436
  415.6 35.3 %copy-start.7 = (bf16[2,256,768]{2,1,0:T(8,128)(2,1)S(1)}, bf16[2,256,768]{2,1,0:T(8,128)(2,1)}, u32[]{:S(2)}) copy-start(bf16[2,256,768]{2,1,0:T(8,128)(2,1)} %get-tuple-element.46) | copy-start | bytes 2359300
  448.5 12.7 %copy-start.9 = (f32[64]{0:T(128)}, f32[64]{0:T(128)S(1)}, u32[]{:S(2)}) copy-start(f32[64]{0:T(128)S(1)} %get-tuple-element.117) | copy-start | bytes 772
  454.4 4.7 %copy-start.4 = (bf16[2,256,1024]{2,1,0:T(8,128)(2,1)S(1)}, bf16[2,256,1024]{2,1,0:T(8,128)(2,1)}, u32[]{:S(2)}) copy-start(bf16[2,256,1024]{2,1,0:T(8,128)(2,1)} %get-tuple-element.49) | copy-start | bytes 3145732

commit v4 on v3

--- a/solution.py
+++ b/solution.py
@@ -446,7 +446,9 @@
     comm = []
     for index in range(2, n_w):
         comm += [starts[index], lasts[index - 1]]
-    comm += [work for more in rows[1:] for work in more[2:]] + [lasts[-1]]
+    comm = comm[:2] + [work for more in rows[1:] for work in more[2:]] + comm[2:] + [lasts[-1]]
+    while len(comm) > 4:
+        comm.pop(0)()
     lines[0].finish()
     spreads[0].finish()
     if fused:

time: 471 us -> 463 us (0.983)
  Pallas kernels: 367 us -> 360 us
    pallas_call x1, Pallas kernels: 195 us -> 184 us  [gather_call(): pl.pallas_call(functools.partial(gather_kernel, len(acts), len(w_srcs), f...]
where the time goes in v4:
time: 463 us; the launch traced here: 455 us
  Pallas kernels  360 us (78%)
  matrix products  50.1 us (11%)
  local copies, waits for them, and re-layouts  32.1 us (7%)
  other arithmetic  11.5 us (2%)
    pallas_call x1, Pallas kernels, gather_call(): pl.pallas_call(functools.partial(gather_kernel, len(acts), len(w_srcs), f...  184 us
    pallas_call x1, Pallas kernels, reduce_call(): pl.pallas_call(functools.partial(reduce_kernel, len(part_shapes), len(gra...  152 us
    pallas_call x1, Pallas kernels, small_call(): pl.pallas_call(functools.partial(small_kernel, f_size, c_size), out_shape...  24.1 us
    dot_general x3, matrix products, weight_grad(): lax.dot_general(left, right, contract_first, preferred_element_type=F32)  19.1 us

profile of v4, /device:TPU:0, one launch (start us, length us, event | category | flops | bytes accessed | tf_op | source)
XLA Modules:
  0.0 455.4 jit_solution(1095731602330943071)
XLA Ops:
  3.8 1.2 convert_reduce_fusion
  5.0 1.3 fusion.15
  8.5 1.8 copy.44
  10.3 1.4 copy.39
  11.7 1.2 copy.45.refs_3_
  13.4 1.3 copy.42
  14.7 2.3 copy.43
  17.0 184.3 %gather_0.1 = (bf16[8,128,2048]{2,1,0:T(8,128)(2,1)}, bf16[8,128,2048]{2,1,0:T(8,128)(2,1)}, bf16[32,16,128]{2,1,0:T(8,128)(2,1)}, bf16[2,4,256,768]{3,2,1,0:T(8...) custom-call(bf16[128,2048]{1,0:T(8,128)(2,1)} %bitcast.83, ...), custom_call_target="tpu_custom_call" | custom-call | tf_op jit(solution)/shard_map/gather_0/pallas_call | solution.py:513
  201.3 1.1 slice.40
  202.4 1.2 convert_reduce_fusion.2
  203.7 4.5 convolution_convert_fusion.3.refs_8_
  208.2 2.3 convolution_convert_fusion.2
  210.6 1.5 copy-done.10
  212.1 4.5 fusion.28
  216.6 7.0 %fusion.25 = (f32[1024]{0:T(1024)S(1)}, bf16[1024,1024]{1,0:T(8,128)(2,1)S(1)}) fusion(f32[1024,1024]{1,0:T(8,128)S(1)} %fusion.28, f32[1024]{0:T(1024)S(1)} %dynamic-slice_convert_fusion, bf16[1024,2048]{1,0:T(8,128)(2,1)S(1)} %bitcast.124, bf16[2048,1024]{1,0:T(8,128)(2,1)S(1)} %bitcast.119), kind=kOutput, calls=%fused_computation.64 | convolution fusion | flops 4316986368 | bytes 14688256 | tf_op jit(solution)/shard_map/dot_general | solution.py:1359
  224.1 10.3 %convolution_convert_fusion.1 = bf16[2048,1024]{1,0:T(8,128)(2,1)} fusion(bf16[1024,2048]{1,0:T(8,128)(2,1)} %bitcast.122, f32[1024,1024]{1,0:T(8,128)} %copy-done.15, f32[1024]{0:T(1024)S(1)} %dynamic-slice_convert_fusion), kind=kOutput, calls=%fused_computation.11 | convolution fusion | flops 4307550208 | bytes 12587008 | tf_op jit(solution)/shard_map/dot_general | solution.py:1364
  234.4 4.9 %fusion.24 = f32[1024,2048]{1,0:T(8,128)S(1)} fusion(bf16[2048,1024]{1,0:T(8,128)(2,1)S(1)} %bitcast.120, f32[1024,1024]{1,0:T(8,128)S(1)} %copy-done.16, f32[1024]{0:T(1024)S(1)} %dynamic-slice_convert_fusion), kind=kOutput, calls=%fused_computation.63 | convolution fusion | flops 4305453056 | bytes 16781312 | tf_op jit(solution)/shard_map/dot_general | solution.py:1357
  239.4 3.2 add_convert_fusion
  242.6 6.8 %fusion.29.refs_14_ = f32[8,128,2048]{2,1,0:T(8,128)} fusion(bf16[8,128,1024]{2,1,0:T(8,128)(2,1)S(1)} %bitcast.125, bf16[2048,1024,1]{1,0,2:T(8,128)(2,1)S(1)} %bitcast.118), kind=kOutput, calls=%fused_computation.68 | convolution fusion | flops 4294967296 | bytes 14680064 | tf_op jit(solution)/shard_map/dot_general | solution.py:1371
  249.4 6.4 %convolution_convert_fusion = bf16[2048,1024]{1,0:T(8,128)(2,1)} fusion(bf16[1024,2048]{1,0:T(8,128)(2,1)S(1)} %bitcast.92, bf16[1024,1024]{1,0:T(8,128)(2,1)S(1)} %get-tuple-element.79), kind=kOutput, calls=%fused_computation.10 | convolution fusion | flops 4297064448 | bytes 10485760 | tf_op jit(solution)/shard_map/dot_general | solution.py:1364
  255.9 151.9 %reduce_2.1 = (f32[128,2048]{1,0:T(8,128)}, f32[128,2048]{1,0:T(8,128)}, bf16[2,256,1024]{2,1,0:T(8,128)(2,1)}, bf16[2,256,1024]{2,1,0:T(8,128)(2,1)}, bf16[2,25...) custom-call(bf16[8,128,2048]{2,1,0:T(8,128)(2,1)} %bitcast.82, ...), custom_call_target="tpu_custom_call" | custom-call | tf_op jit(solution)/shard_map/reduce_2/pallas_call | solution.py:991
  408.8 1.8 fusion.14
  410.6 3.5 convert_reduce_fusion.1
  415.1 24.1 %small_4.1 = f32[8,128]{1,0:T(8,128)} custom-call(f32[32,8,128]{2,1,0:T(8,128)} %bitcast.106), custom_call_target="tpu_custom_call" | custom-call | tf_op jit(solution)/shard_map/small_4/pallas_call | solution.py:1059
  439.1 1.2 slice_bitcast_fusion
  440.4 1.4 fusion.27
  443.1 1.0 copy.49
  444.6 1.6 copy.52
  446.2 1.5 convert_bitcast_fusion.1
  447.7 1.8 copy.50
  449.5 2.9 copy.53
  452.6 1.8 copy.51
  (80 shorter events, 11.0 us)
Async XLA Ops:
  0.6 12.3 %copy-start.6 = (bf16[256,2048]{1,0:T(8,128)(2,1)S(1)}, bf16[256,2048]{1,0:T(8,128)(2,1)}, u32[]{:S(2)}) copy-start(bf16[256,2048]{1,0:T(8,128)(2,1)} %param.21) | copy-start | bytes 3145732
  201.3 6.9 %copy-start.3 = (bf16[1024,256]{1,0:T(8,128)(2,1)S(1)}, bf16[1024,256]{1,0:T(8,128)(2,1)}, u32[]{:S(2)}) copy-start(bf16[1024,256]{1,0:T(8,128)(2,1)} %get-tuple-element.31.refs_7_) | copy-start | bytes 1572868
  201.3 6.9 %copy-start.14 = (bf16[8,128,2048]{2,1,0:T(8,128)(2,1)S(1)}, bf16[8,128,2048]{2,1,0:T(8,128)(2,1)}, u32[]{:S(2)}) copy-start(bf16[8,128,2048]{2,1,0:T(8,128)(2,1)} %get-tuple-element.37) | copy-start | bytes 12582916
  208.2 2.4 copy-start.1
  208.2 3.8 copy-start.10
  212.1 4.5 copy-start.12
  216.6 7.0 %copy-start.15 = (f32[1024,1024]{1,0:T(8,128)}, f32[1024,1024]{1,0:T(8,128)S(1)}, u32[]{:S(2)}) copy-start(f32[1024,1024]{1,0:T(8,128)S(1)} %fusion.28) | copy-start | bytes 12582916
  224.1 10.3 %copy-start.13 = (bf16[2,4,256,1024]{3,2,1,0:T(8,128)(2,1)S(1)}, bf16[2,4,256,1024]{3,2,1,0:T(8,128)(2,1)}, u32[]{:S(2)}) copy-start(bf16[2,4,256,1024]{3,2,1,0:T(8,128)(2,1)} %get-tuple-element.36) | copy-start | bytes 12582916
  224.1 10.3 %copy-start.16 = (f32[1024,1024]{1,0:T(8,128)S(1)}, f32[1024,1024]{1,0:T(8,128)}, u32[]{:S(2)}) copy-start(f32[1024,1024]{1,0:T(8,128)} %copy-done.15) | copy-start | bytes 12582916
  234.4 4.9 %copy-start.5 = (bf16[2,4,256,256]{3,2,1,0:T(8,128)(2,1)S(1)}, bf16[2,4,256,256]{3,2,1,0:T(8,128)(2,1)}, u32[]{:S(2)}) copy-start(bf16[2,4,256,256]{3,2,1,0:T(8,128)(2,1)} %get-tuple-element.32) | copy-start | bytes 3145732
  239.4 3.2 copy-start.11
  242.6 6.8 %copy-start.2 = (bf16[8,128,2048]{2,1,0:T(8,128)(2,1)S(1)}, bf16[8,128,2048]{2,1,0:T(8,128)(2,1)}, u32[]{:S(2)}) copy-start(bf16[8,128,2048]{2,1,0:T(8,128)(2,1)} %get-tuple-element.33) | copy-start | bytes 12582916
  255.9 152.9 %copy-start = (bf16[1,128,2048]{2,1,0:T(8,128)(2,1)S(1)}, bf16[1,128,2048]{2,1,0:T(8,128)(2,1)}, u32[]{:S(2)}) copy-start(bf16[1,128,2048]{2,1,0:T(8,128)(2,1)} %param.14) | copy-start | bytes 1572868
  407.8 35.3 %copy-start.8 = (bf16[2,256,256]{2,1,0:T(8,128)(2,1)S(1)}, bf16[2,256,256]{2,1,0:T(8,128)(2,1)}, u32[]{:S(2)}) copy-start(bf16[2,256,256]{2,1,0:T(8,128)(2,1)} %get-tuple-element.47) | copy-start | bytes 786436
  408.8 35.3 %copy-start.7 = (bf16[2,256,768]{2,1,0:T(8,128)(2,1)S(1)}, bf16[2,256,768]{2,1,0:T(8,128)(2,1)}, u32[]{:S(2)}) copy-start(bf16[2,256,768]{2,1,0:T(8,128)(2,1)} %get-tuple-element.46) | copy-start | bytes 2359300
  441.7 12.7 %copy-start.9 = (f32[64]{0:T(128)}, f32[64]{0:T(128)S(1)}, u32[]{:S(2)}) copy-start(f32[64]{0:T(128)S(1)} %get-tuple-element.117) | copy-start | bytes 772
  447.6 4.7 %copy-start.4 = (bf16[2,256,1024]{2,1,0:T(8,128)(2,1)S(1)}, bf16[2,256,1024]{2,1,0:T(8,128)(2,1)}, u32[]{:S(2)}) copy-start(bf16[2,256,1024]{2,1,0:T(8,128)(2,1)} %get-tuple-element.49) | copy-start | bytes 3145732
